TPU v7x, 32 devices: a whole 2x2x4 slice. The times are simulated.
32 devices in a mesh: wave: 16 (over z, y, core), lev: 2 (over x).
Axes of the slice: x: 2, y: 2, z: 4, core: 2. Of those that a mesh axis runs over, the one named last changes fastest.
Arguments:
- control: bfloat16 [2, 256, 256, 2, 512], P(None, 'wave', 'lev'), may hold values from -6 to 6
- wave_of_slot: int32 [256], replicated, may hold values from 0 to 255, each once
- legendre: bfloat16 [256, 256, 256], P('wave', 'lev'), may hold values from -0.375 to 0.375
- vertical: bfloat16 [4, 4, 128, 128], replicated, may hold values from -0.5 to 0.5
- points: int32 [256], P('wave'), may hold values from 128 to 512
- lat_band: int32 [256], P('wave'), may hold values from 0 to 7, never falling along the last dimension, each value on 1 to 64 neighbouring positions
- grid_scale: float32 [8, 512], P(None, 'lev'), may hold values from 0.5 to 2
- obs_weight: bfloat16 [256, 512, 512], P('wave', 'lev'), may hold values from 0.19921875 to 1
Outputs:
- increment: bfloat16 [2, 256, 512, 512], P(None, 'wave', 'lev')
- gradient: bfloat16 [2, 256, 256, 2, 512], P(None, 'wave', 'lev')
Inputs may be any that keep to these rules, and one draw needn't show every extreme that they name: `wave_of_slot`: each zonal wavenumber 0 to 255 stands in exactly one slot. `lat_band`: band numbers never fall from one latitude to the next, and each band covers 1 to 64 latitudes.
All inputs are finite; a program needn't handle non-finite values.
Results may differ from a plain program's by a relative error of at most 0.007.
Values may be sent and summed in bfloat16 or wider, within the bound.
A program may use at most 192 MiB of HBM per device.

v0:
```python
import functools
import math

import jax
import jax.numpy as jnp
from jax import lax
from jax.experimental import pallas as pl
from jax.experimental.pallas import tpu as pltpu
from jax.sharding import PartitionSpec as P

WAVES = 256
LONGITUDES = 512
LEVELS = 128
VARIABLES = 4
COV_BANDS = 4


def fourier_table(wave_ids, lat_points):
    lon_index = jnp.arange(LONGITUDES, dtype=jnp.int32)
    remainder = wave_ids[None, :, None] * lon_index[None, None, :] % lat_points[:, None, None]
    angles = (
        2.0
        * math.pi
        * remainder.astype(jnp.float32)
        / lat_points.astype(jnp.float32)[:, None, None]
    )
    factor = jnp.where(wave_ids == 0, 1.0, 2.0).astype(jnp.float32) / math.sqrt(4.0 * WAVES)
    inside = lon_index[None, None, :] < lat_points[:, None, None]
    cosine = jnp.where(inside, factor[None, :, None] * jnp.cos(angles), 0.0)
    sine = jnp.where(inside, -factor[None, :, None] * jnp.sin(angles), 0.0)
    return jnp.stack([cosine, sine], axis=2).astype(jnp.bfloat16)


def vertical_apply(field, vertical, live_rows, band_of, forward):
    members, slots, rows_dev = (field.shape[0], field.shape[1], field.shape[2])
    shaped = field.reshape(members, slots, rows_dev, 2, VARIABLES, LEVELS)
    form = "eskpam,alm->eskpal" if forward else "eskpal,alm->eskpam"
    summed = jnp.zeros(shaped.shape, jnp.float32)
    for index_band in range(COV_BANDS):
        partial_value = jnp.einsum(
            form, shaped, vertical[index_band], preferred_element_type=jnp.float32
        )
        chosen = live_rows & (band_of == index_band)
        summed = summed + jnp.where(chosen[None, :, :, None, None, None], partial_value, 0.0)
    return summed.reshape(field.shape).astype(jnp.bfloat16)


def to_bands(values):
    return lax.all_to_all(values, "wave", split_axis=2, concat_axis=1, tiled=True)


def shards_plain(control, wave_of_slot, legendre, vertical, points, lat_band, grid_scale, obs_weight):
    members, slots, rows_dev = (control.shape[0], control.shape[1], control.shape[2])
    slot_start = lax.axis_index("wave") * slots
    row_start = lax.axis_index("lev") * rows_dev
    own_waves = lax.dynamic_slice_in_dim(wave_of_slot, slot_start, slots)
    row_index = row_start + jnp.arange(rows_dev, dtype=jnp.int32)
    totals_n = own_waves[:, None] + row_index[None, :]
    live_rows = totals_n <= WAVES - 1
    band_of = jnp.minimum(totals_n * COV_BANDS // WAVES, COV_BANDS - 1)
    spectral = vertical_apply(control, vertical, live_rows, band_of, True)
    columns = lax.all_to_all(spectral, "lev", split_axis=4, concat_axis=2, tiled=True)
    col_dev = columns.shape[4]
    width = 2 * col_dev
    all_rows = columns.shape[2]
    columns = columns.reshape(members, slots, all_rows, width)
    coeffs = jnp.einsum(
        "skt,eskq->estq",
        lax.all_gather(legendre, "lev", axis=1, tiled=True),
        columns,
        preferred_element_type=jnp.float32,
    )
    coeffs = coeffs.astype(jnp.bfloat16)
    by_lat = to_bands(coeffs)
    wave_count = by_lat.shape[1]
    lat_dev = by_lat.shape[2]
    by_lat = by_lat.reshape(members, wave_count, lat_dev, 2, col_dev)
    fourier = fourier_table(wave_of_slot, points)
    synthesis = jnp.einsum("tspj,estpc->etcj", fourier, by_lat, preferred_element_type=jnp.float32)
    chooser = (
        lat_band[:, None] == jnp.arange(grid_scale.shape[0], dtype=jnp.int32)[None, :]
    ).astype(jnp.float32)
    lat_scale = jnp.dot(chooser, grid_scale, precision=lax.Precision.HIGHEST)
    increment = (synthesis * lat_scale[None, :, :, None]).astype(jnp.bfloat16)
    weighted = (
        increment.astype(jnp.float32) * obs_weight.astype(jnp.float32) * lat_scale[None, :, :, None]
    ).astype(jnp.bfloat16)
    adjoint_fourier = jnp.einsum(
        "tspj,etcj->etspc", fourier, weighted, preferred_element_type=jnp.float32
    )
    adjoint_fourier = adjoint_fourier.astype(jnp.bfloat16).reshape(
        members, lat_dev, wave_count, width
    )
    band_rows = to_bands(adjoint_fourier)
    adjoint_coeffs = jnp.einsum(
        "skt,etsq->eskq",
        lax.all_gather(legendre, "lev", axis=1, tiled=True),
        band_rows,
        preferred_element_type=jnp.float32,
    )
    adjoint_coeffs = adjoint_coeffs.astype(jnp.bfloat16).reshape(
        members, slots, all_rows, 2, col_dev
    )
    rows_back = lax.all_to_all(adjoint_coeffs, "lev", split_axis=2, concat_axis=4, tiled=True)
    gradient = vertical_apply(rows_back, vertical, live_rows, band_of, False)
    return (increment, gradient)


MESH = pl.DeviceIdType.MESH
VMEM_BYTES = 64000 * 1024


def enter(n_wave, n_lev):
    me_w, me_l = lax.axis_index("wave"), lax.axis_index("lev")
    barrier = pltpu.get_barrier_semaphore()

    def greet(d, carry):
        peer = lax.rem(me_w + d, n_wave)
        pl.semaphore_signal(barrier, inc=1, device_id=(peer, me_l), device_id_type=MESH)
        return carry

    lax.fori_loop(1, n_wave, greet, 0)
    for d in range(1, n_lev):
        peer = lax.rem(me_l + d, n_lev)
        pl.semaphore_signal(barrier, inc=1, device_id=(me_w, peer), device_id_type=MESH)
    pl.semaphore_wait(barrier, n_wave + n_lev - 2)
    return me_w, me_l


def band_masks(wave, row0, rows, waves):
    total = wave + row0 + lax.broadcasted_iota(jnp.int32, (rows, LEVELS), 0)
    width = waves // COV_BANDS
    masks = []
    for b in range(COV_BANDS):
        hit = (total >= b * width) & (total < (b + 1) * width)
        masks.append(jnp.where(hit, 1.0, 0.0).astype(jnp.bfloat16))
    return masks


def banded_dot(x, masks, matrix):
    stacked = jnp.concatenate([x * mask for mask in masks], axis=1)
    return jnp.dot(stacked, matrix, preferred_element_type=jnp.float32).astype(jnp.bfloat16)


def forward_kernel(n_wave, n_lev, waves, waves_ref, x_ref, l_ref, v_ref, out_ref, full_ref,
                   full, l_send, l_recv, full_sem, spec, away, coef, wsend, x_send, x_recv, w_send, w_recv, own_sem):
    chunks, slots, rows, _ = x_ref.shape
    lats = l_ref.shape[2] // n_wave
    per = v_ref.shape[0] // n_lev
    me_w, me_l = enter(n_wave, n_lev)
    row0 = me_l * rows

    def lev_copy(q, d):
        peer = lax.rem(me_l + d, n_lev)
        return pltpu.make_async_remote_copy(
            src_ref=away.at[q, d - 1], dst_ref=spec.at[q, me_l],
            send_sem=x_send.at[q, d - 1], recv_sem=x_recv.at[q, d - 1],
            device_id=(me_w, peer), device_id_type=MESH)

    def wave_copy(q, d):
        peer = lax.rem(me_w + d, n_wave)
        return pltpu.make_async_remote_copy(
            src_ref=wsend.at[q, peer], dst_ref=out_ref.at[q, me_w],
            send_sem=w_send.at[q, d - 1], recv_sem=w_recv.at[q, d - 1],
            device_id=(peer, me_l), device_id_type=MESH)

    def own_copy(q):
        return pltpu.make_async_copy(wsend.at[q, me_w], out_ref.at[q, me_w], own_sem.at[q])

    def table_copy(d):
        peer = lax.rem(me_l + d, n_lev)
        return pltpu.make_async_remote_copy(
            src_ref=l_ref, dst_ref=full.at[me_l],
            send_sem=l_send.at[d - 1], recv_sem=l_recv.at[d - 1],
            device_id=(me_w, peer), device_id_type=MESH)

    for d in range(1, n_lev):
        table_copy(d).start()
    full[me_l] = l_ref[...]
    keep = pltpu.make_async_copy(full, full_ref, full_sem)

    for q in range(chunks):
        def vertical_slot(s, carry):
            masks = band_masks(waves_ref[s], row0, rows, waves)
            for d in list(range(1, n_lev)) + [0]:
                half = lax.rem(me_l + d, n_lev)
                for i in range(per):
                    a = half * per + i
                    x = x_ref[q, s, :, pl.ds(pl.multiple_of(a * LEVELS, LEVELS), LEVELS)]
                    y = banded_dot(x, masks, v_ref[a])
                    if d == 0:
                        spec[q, me_l, s, :, i * LEVELS:(i + 1) * LEVELS] = y
                    else:
                        away[q, d - 1, s, :, i * LEVELS:(i + 1) * LEVELS] = y
            return carry

        lax.fori_loop(0, slots, vertical_slot, 0)
        for d in range(1, n_lev):
            lev_copy(q, d).start()

    for d in range(1, n_lev):
        table_copy(d).wait()
    keep.start()
    for q in range(chunks):
        for d in range(1, n_lev):
            lev_copy(q, d).wait_recv()

        def legendre_slot(s, carry):
            field = jnp.concatenate([spec[q, l, s] for l in range(n_lev)], axis=0)
            table = jnp.concatenate([full[l, s] for l in range(n_lev)], axis=0)
            coef[s] = lax.dot_general(table, field, (((0,), (0,)), ((), ())), preferred_element_type=jnp.float32)
            return carry

        lax.fori_loop(0, slots, legendre_slot, 0)

        def turn(w, carry):
            for t in range(lats):
                wsend[q, w, t] = coef[:, w * lats + t, :].astype(jnp.bfloat16)
            return carry

        lax.fori_loop(0, n_wave, turn, 0)

        def send(d, carry):
            wave_copy(q, d).start()
            return carry

        lax.fori_loop(1, n_wave, send, 0)
        own_copy(q).start()

    for q in range(chunks):
        def finish(d, carry):
            wave_copy(q, d).wait()
            return carry

        lax.fori_loop(1, n_wave, finish, 0)
        own_copy(q).wait()
        for d in range(1, n_lev):
            lev_copy(q, d).wait_send()
    keep.wait()


def adjoint_kernel(n_wave, n_lev, waves, waves_ref, a_ref, l_ref, v_ref, out_ref,
                   land, fine, away, back, w_send, w_recv, x_send, x_recv):
    chunks, _, lats, slots, cols = a_ref.shape
    rows = out_ref.shape[2]
    per = v_ref.shape[0] // n_lev
    me_w, me_l = enter(n_wave, n_lev)
    row0 = me_l * rows

    def wave_copy(q, d):
        peer = lax.rem(me_w + d, n_wave)
        return pltpu.make_async_remote_copy(
            src_ref=a_ref.at[q, peer], dst_ref=land.at[q, me_w],
            send_sem=w_send.at[q, d - 1], recv_sem=w_recv.at[q, d - 1],
            device_id=(peer, me_l), device_id_type=MESH)

    def lev_copy(q, d):
        peer = lax.rem(me_l + d, n_lev)
        return pltpu.make_async_remote_copy(
            src_ref=away.at[q, d - 1], dst_ref=back.at[q, me_l],
            send_sem=x_send.at[q, d - 1], recv_sem=x_recv.at[q, d - 1],
            device_id=(me_w, peer), device_id_type=MESH)

    for q in range(chunks):
        def send(d, carry):
            wave_copy(q, d).start()
            return carry

        lax.fori_loop(1, n_wave, send, 0)
        land[q, me_w] = a_ref[q, me_w]

    for q in range(chunks):
        def arrive(d, carry):
            wave_copy(q, d).wait_recv()
            return carry

        lax.fori_loop(1, n_wave, arrive, 0)

        def widen(w, carry):
            base = pl.multiple_of(w * lats, lats)
            fine[pl.ds(base, lats)] = land[q, w].astype(jnp.float32)
            return carry

        lax.fori_loop(0, n_wave, widen, 0)

        def legendre_slot(s, carry):
            field = fine[:, s, :].astype(jnp.bfloat16)
            for d in range(n_lev):
                half = lax.rem(me_l + d, n_lev)
                table = l_ref[half, s]
                y = jnp.dot(table, field, preferred_element_type=jnp.float32).astype(jnp.bfloat16)
                if d == 0:
                    back[q, me_l, s] = y
                else:
                    away[q, d - 1, s] = y
            return carry

        lax.fori_loop(0, slots, legendre_slot, 0)
        for d in range(1, n_lev):
            lev_copy(q, d).start()

    for q in range(chunks):
        for d in range(1, n_lev):
            lev_copy(q, d).wait()

        def vertical_slot(s, carry):
            masks = band_masks(waves_ref[s], row0, rows, waves)
            for l in range(n_lev):
                for i in range(per):
                    a = l * per + i
                    x = back[q, l, s, :, i * LEVELS:(i + 1) * LEVELS]
                    out_ref[q, s, :, a * LEVELS:(a + 1) * LEVELS] = banded_dot(x, masks, v_ref[a])
            return carry

        lax.fori_loop(0, slots, vertical_slot, 0)

    for q in range(chunks):
        def drain(d, carry):
            wave_copy(q, d).wait_send()
            return carry

        lax.fori_loop(1, n_wave, drain, 0)


SIN_TERMS = [(-1.0) ** i * (2.0 * math.pi) ** (2 * i + 1) / math.factorial(2 * i + 1) for i in range(10)]
COS_TERMS = [(-1.0) ** i * (2.0 * math.pi) ** (2 * i) / math.factorial(2 * i) for i in range(10)]


def horner(terms, square):
    value = jnp.full_like(square, terms[-1])
    for term in terms[-2::-1]:
        value = value * square + term
    return value


def grid_kernel(waves_ref, points_ref, x_ref, scale_ref, weight_ref, inc_ref, adj_ref, table):
    members, _, cols, longs = inc_ref.shape
    waves = waves_ref.shape[0]
    points = points_ref[pl.program_id(0)]
    n = points.astype(jnp.float32)
    piece = 32
    inverse = 1.0 / jnp.full((1, longs), n, jnp.float32)
    lane = lax.broadcasted_iota(jnp.int32, (1, longs), 1)
    inside = jnp.where(lane < points, 1.0, 0.0) / math.sqrt(4.0 * waves)

    def build(i, carry):
        base = pl.multiple_of(i * piece, piece)
        wave = waves_ref[pl.ds(base, piece), :]
        product = wave * lane.astype(jnp.float32)
        turns = jnp.floor(product * inverse + 0.5)
        x = (product - turns * n) * inverse
        square = x * x
        gain = jnp.where(wave == 0.0, 1.0, 2.0) * inside
        table[pl.ds(base, piece), :] = (gain * horner(COS_TERMS, square)).astype(jnp.bfloat16)
        sine = (-gain) * (x * horner(SIN_TERMS, square))
        table[pl.ds(pl.multiple_of(waves + base, piece), piece), :] = sine.astype(jnp.bfloat16)
        return carry

    lax.fori_loop(0, waves // piece, build, 0)
    scale = scale_ref[0]
    for e in range(members):
        coeffs = jnp.concatenate([x_ref[2 * e + p, :, 0].reshape(waves, cols) for p in range(2)], axis=0)
        synthesis = lax.dot_general(coeffs, table[...], (((0,), (0,)), ((), ())),
                                    preferred_element_type=jnp.float32)
        increment = (synthesis * scale).astype(jnp.bfloat16)
        inc_ref[e, 0] = increment
        weighted = (increment.astype(jnp.float32) * weight_ref[0].astype(jnp.float32) * scale)
        adjoint = lax.dot_general(table[...], weighted.astype(jnp.bfloat16), (((1,), (1,)), ((), ())),
                                  preferred_element_type=jnp.float32).astype(jnp.bfloat16)
        for p in range(2):
            part = adjoint[p * waves:(p + 1) * waves]
            adj_ref[2 * e + p, :, 0] = part.reshape(adj_ref.shape[1], adj_ref.shape[3], cols)


def shards_kernels(n_wave, n_lev, control, wave_of_slot, legendre, vertical, points, lat_band, grid_scale, obs_weight):
    members, slots, rows = control.shape[:3]
    waves = wave_of_slot.shape[0]
    variables = vertical.shape[1]
    columns = control.shape[4]
    cols = columns // n_lev
    lats, _, longs = obs_weight.shape
    chunks = 2 * members
    bf16, f32 = jnp.bfloat16, jnp.float32
    own_waves = lax.dynamic_slice_in_dim(wave_of_slot, lax.axis_index("wave") * slots, slots)
    x = control.transpose(0, 3, 1, 2, 4).reshape(chunks, slots, rows, columns)
    stack_f = vertical.transpose(1, 0, 3, 2).reshape(variables, COV_BANDS * LEVELS, LEVELS)
    stack_g = vertical.transpose(1, 0, 2, 3).reshape(variables, COV_BANDS * LEVELS, LEVELS)
    vmem = pl.BlockSpec(memory_space=pltpu.VMEM)
    smem = pl.BlockSpec(memory_space=pltpu.SMEM)
    dma = pltpu.SemaphoreType.DMA
    by_lat, table = pl.pallas_call(
        functools.partial(forward_kernel, n_wave, n_lev, waves),
        out_shape=[
            jax.ShapeDtypeStruct((chunks, n_wave, lats, slots, cols), bf16),
            jax.ShapeDtypeStruct((n_lev, *legendre.shape), bf16),
        ],
        in_specs=[smem, vmem, vmem, vmem],
        out_specs=[pl.BlockSpec(memory_space=pl.ANY)] * 2,
        scratch_shapes=[
            pltpu.VMEM((n_lev, *legendre.shape), bf16),
            dma((n_lev - 1,)), dma((n_lev - 1,)), dma,
            pltpu.VMEM((chunks, n_lev, slots, rows, cols), bf16),
            pltpu.VMEM((chunks, n_lev - 1, slots, rows, cols), bf16),
            pltpu.VMEM((slots, n_wave * lats, cols), f32),
            pltpu.VMEM((chunks, n_wave, lats, slots, cols), bf16),
            dma((chunks, n_lev - 1)), dma((chunks, n_lev - 1)),
            dma((chunks, n_wave - 1)), dma((chunks, n_wave - 1)), dma((chunks,)),
        ],
        compiler_params=pltpu.CompilerParams(collective_id=0, has_side_effects=True, vmem_limit_bytes=VMEM_BYTES),
        name="forward",
    )(own_waves, x, legendre, stack_f)
    chooser = (
        lat_band[:, None] == jnp.arange(grid_scale.shape[0], dtype=jnp.int32)[None, :]
    ).astype(f32)
    lat_scale = jnp.dot(chooser, grid_scale, precision=lax.Precision.HIGHEST)
    field_spec = pl.BlockSpec((chunks, n_wave, 1, slots, cols), lambda t: (0, 0, t, 0, 0))
    increment, adjoint = pl.pallas_call(
        grid_kernel,
        grid=(lats,),
        out_shape=[
            jax.ShapeDtypeStruct((members, lats, cols, longs), bf16),
            jax.ShapeDtypeStruct((chunks, n_wave, lats, slots, cols), bf16),
        ],
        in_specs=[
            pl.BlockSpec((waves, 1), lambda t: (0, 0)),
            smem,
            field_spec,
            pl.BlockSpec((1, cols, 1), lambda t: (t, 0, 0)),
            pl.BlockSpec((1, cols, longs), lambda t: (t, 0, 0)),
        ],
        out_specs=[pl.BlockSpec((members, 1, cols, longs), lambda t: (0, t, 0, 0)), field_spec],
        scratch_shapes=[pltpu.VMEM((2 * waves, longs), bf16)],
        compiler_params=pltpu.CompilerParams(vmem_limit_bytes=VMEM_BYTES // 2),
        name="grid",
    )(wave_of_slot.astype(f32)[:, None], points, by_lat, lat_scale[:, :, None], obs_weight)
    gradient = pl.pallas_call(
        functools.partial(adjoint_kernel, n_wave, n_lev, waves),
        out_shape=jax.ShapeDtypeStruct((chunks, slots, rows, columns), bf16),
        in_specs=[smem, vmem, vmem, vmem],
        out_specs=vmem,
        scratch_shapes=[
            pltpu.VMEM((chunks, n_wave, lats, slots, cols), bf16),
            pltpu.VMEM((n_wave * lats, slots, cols), f32),
            pltpu.VMEM((chunks, n_lev - 1, slots, rows, cols), bf16),
            pltpu.VMEM((chunks, n_lev, slots, rows, cols), bf16),
            dma((chunks, n_wave - 1)), dma((chunks, n_wave - 1)),
            dma((chunks, n_lev - 1)), dma((chunks, n_lev - 1)),
        ],
        compiler_params=pltpu.CompilerParams(collective_id=1, has_side_effects=True, vmem_limit_bytes=VMEM_BYTES),
        name="adjoint",
    )(own_waves, adjoint, table, stack_g)
    gradient = gradient.reshape(members, 2, slots, rows, columns).transpose(0, 2, 3, 1, 4)
    return (increment, gradient)


def shards(n_wave, n_lev, *arrays):
    slots, rows, columns = arrays[0].shape[1], arrays[0].shape[2], arrays[0].shape[4]
    whole_tiles = slots % 16 == 0 and rows % 128 == 0 and columns % (n_lev * LEVELS) == 0
    if whole_tiles and n_lev > 1:
        return shards_kernels(n_wave, n_lev, *arrays)
    return shards_plain(*arrays)


def solution(mesh):
    in_specs = (
        P(None, "wave", "lev", None, None),
        P(),
        P("wave", "lev", None),
        P(),
        P("wave"),
        P("wave"),
        P(None, "lev"),
        P("wave", "lev", None),
    )
    out_specs = (P(None, "wave", "lev", None), P(None, "wave", "lev", None, None))
    body = functools.partial(shards, mesh.shape["wave"], mesh.shape["lev"])
    return jax.shard_map(body, mesh=mesh, in_specs=in_specs, out_specs=out_specs, check_vma=False)
```

profile of v0, /device:TPU:29, one launch (start us, length us, event | category | flops | bytes accessed | tf_op | source)
XLA Modules:
  0.0 555.8 jit_solution(13079671333902197970)
XLA Ops:
  0.6 0.0 copy-start
  0.7 1.3 dynamic_slice.3.waves_ref
  1.9 0.0 copy-start.6
  1.9 8.8 %copy.14 = bf16[2,2,16,128,512]{4,3,2,1,0:T(8,128)(2,1)} copy(bf16[2,2,16,128,512]{4,1,3,2,0:T(2,128)(2,1)} %bitcast.16) | data formatting | bytes 16777216 | tf_op jit(solution)/shard_map/transpose | solution.py:385
  10.7 0.0 copy-start.8
  10.7 0.0 copy-start.7
  10.7 0.0 copy-start.5
  10.7 0.0 copy-done.6
  10.7 1.0 copy.15
  11.7 244.6 %forward.1 = (bf16[4,16,16,16,256]{4,3,2,1,0:T(8,128)(2,1)}, bf16[2,16,128,256]{3,2,1,0:T(8,128)(2,1)}) custom-call(s32[16]{0:T(128)} %dynamic_slice.3.waves_ref, bf16[4,16,128,512]{3,2,1,0:T(8,128)(2,1)} %bitcast.15, bf16[16,128,256]{2,1,0:T(8,128)(2,1)} %l_ref.1, bf16[4,512,128]{2,1,0:T(8,128)(2,1)} %bitcast.18), custom_call_target="tpu_custom_call" | custom-call | tf_op jit(solution)/shard_map/forward/pallas_call | solution.py:391
  256.3 0.0 copy-done
  256.3 0.0 copy-done.8
  256.3 0.2 convolution_bitcast_fusion
  256.5 0.6 copy.17.scale_ref
  257.2 0.0 copy-done.7
  257.2 0.1 copy.16.waves_ref
  257.3 0.0 copy-done.5
  257.4 0.0 copy-start.2
  257.4 3.4 copy-done.2
  260.7 0.0 copy-start.4
  260.7 2.2 copy-done.4
  262.9 44.9 %grid.1 = (bf16[2,16,256,512]{3,2,1,0:T(8,128)(2,1)}, bf16[4,16,16,16,256]{4,3,2,1,0:T(8,128)(2,1)S(1)}) custom-call(f32[256,1]{1,0:T(8,128)S(1)} %copy.16.waves_ref, s32[16]{0:T(128)S(1)} %copy-done.5, bf16[4,16,16,16,256]{4,3,2,1,0:T(8,128)(2,1)S(1)} %copy-done.2, f32[16,256,1]{2,1,0:T(8,128)S(1)} %copy.17.scale_ref, bf16[16,256,512]{2,1,0:T(8,128)(2,1)S(1)} %copy-done.4), custom_call_target="tpu_custom_call" | custom-call | tf_op jit(solution)/shard_map/grid/pallas_call | solution.py:417
  307.8 0.0 copy-start.3
  307.8 3.4 copy-done.3
  311.2 0.8 copy.18
  312.1 227.3 %adjoint.1 = bf16[4,16,128,512]{3,2,1,0:T(8,128)(2,1)} custom-call(s32[16]{0:T(128)} %dynamic_slice.3.waves_ref, bf16[4,16,16,16,256]{4,3,2,1,0:T(8,128)(2,1)} %copy-done.3, bf16[2,16,128,256]{3,2,1,0:T(8,128)(2,1)} %get-tuple-element.9.l_ref, bf16[4,512,128]{2,1,0:T(8,128)(2,1)} %bitcast.19), custom_call_target="tpu_custom_call" | custom-call | tf_op jit(solution)/shard_map/adjoint/pallas_call | solution.py:436
  539.3 0.0 copy-start.1
  539.4 16.4 %copy.21 = bf16[2,2,16,128,512]{4,1,3,2,0:T(2,128)(2,1)} copy(bf16[2,2,16,128,512]{4,3,2,1,0:T(8,128)(2,1)} %bitcast.14) | data formatting | bytes 16777216 | tf_op jit(solution)/shard_map/reshape | solution.py:452
  555.8 0.0 copy-done.1
  (1 shorter events, 0.0 us)
Async XLA Ops:
  0.6 255.7 %copy-start = (f32[8,256]{1,0:T(8,128)S(1)}, f32[8,256]{1,0:T(8,128)}, u32[]{:S(2)}) copy-start(f32[8,256]{1,0:T(8,128)} %param.14) | copy-start | bytes 24580
  1.9 8.8 %copy-start.6 = (bf16[4,4,128,128]{3,2,1,0:T(8,128)(2,1)S(1)}, bf16[4,4,128,128]{3,2,1,0:T(8,128)(2,1)}, u32[]{:S(2)}) copy-start(bf16[4,4,128,128]{3,2,1,0:T(8,128)(2,1)} %param.11) | copy-start | bytes 1572868
  10.7 245.6 %copy-start.8 = (s32[16]{0:T(128)S(1)}, s32[16]{0:T(128)}, u32[]{:S(2)}) copy-start(s32[16]{0:T(128)} %param.13) | copy-start | bytes 196
  10.7 246.5 %copy-start.7 = (s32[256]{0:T(256)S(1)}, s32[256]{0:T(256)}, u32[]{:S(2)}) copy-start(s32[256]{0:T(256)} %param.9) | copy-start | bytes 3076
  10.7 246.6 %copy-start.5 = (s32[16]{0:T(128)S(1)}, s32[16]{0:T(128)}, u32[]{:S(2)}) copy-start(s32[16]{0:T(128)} %points_ref.1) | copy-start | bytes 196
  257.4 3.4 copy-start.2
  260.7 2.2 copy-start.4
  307.8 3.4 copy-start.3
  539.3 16.5 %copy-start.1 = (f32[8,256]{1,0:T(8,128)S(1)}, f32[8,256]{1,0:T(8,128)}, u32[]{:S(2)}) copy-start(f32[8,256]{1,0:T(8,128)} %param.14) | copy-start | bytes 24580
where the time goes:
time: 556 us
  Pallas kernels  517 us (93%)
  local copies, waits for them, and re-layouts  38.1 us (7%)
    pallas_call x1, Pallas kernels, shards_kernels(): pl.pallas_call(functools.partial(forward_kernel, n_wave, n_lev, waves), o...  245 us
    pallas_call x1, Pallas kernels, shards_kernels(): pl.pallas_call(functools.partial(adjoint_kernel, n_wave, n_lev, waves), o...  227 us
    pallas_call x1, Pallas kernels, shards_kernels(): pl.pallas_call(grid_kernel, grid=(lats,), out_shape=[jax.ShapeDtypeStruct...  44.9 us
    reshape x1, local copies, waits for them, and re-layouts, shards_kernels(): gradient.reshape(members, 2, slots, rows, columns).transpose(0, 2, 3, 1, 4)  16.4 us

commit v1 on v0

v1 whole, which is shorter than its diff:
```python
import functools
import math

import jax
import jax.numpy as jnp
from jax import lax
from jax.experimental import pallas as pl
from jax.experimental.pallas import tpu as pltpu
from jax.sharding import PartitionSpec as P

WAVES = 256
LONGITUDES = 512
LEVELS = 128
VARIABLES = 4
COV_BANDS = 4


def fourier_table(wave_ids, lat_points):
    lon_index = jnp.arange(LONGITUDES, dtype=jnp.int32)
    remainder = wave_ids[None, :, None] * lon_index[None, None, :] % lat_points[:, None, None]
    angles = (
        2.0
        * math.pi
        * remainder.astype(jnp.float32)
        / lat_points.astype(jnp.float32)[:, None, None]
    )
    factor = jnp.where(wave_ids == 0, 1.0, 2.0).astype(jnp.float32) / math.sqrt(4.0 * WAVES)
    inside = lon_index[None, None, :] < lat_points[:, None, None]
    cosine = jnp.where(inside, factor[None, :, None] * jnp.cos(angles), 0.0)
    sine = jnp.where(inside, -factor[None, :, None] * jnp.sin(angles), 0.0)
    return jnp.stack([cosine, sine], axis=2).astype(jnp.bfloat16)


def vertical_apply(field, vertical, live_rows, band_of, forward):
    members, slots, rows_dev = (field.shape[0], field.shape[1], field.shape[2])
    shaped = field.reshape(members, slots, rows_dev, 2, VARIABLES, LEVELS)
    form = "eskpam,alm->eskpal" if forward else "eskpal,alm->eskpam"
    summed = jnp.zeros(shaped.shape, jnp.float32)
    for index_band in range(COV_BANDS):
        partial_value = jnp.einsum(
            form, shaped, vertical[index_band], preferred_element_type=jnp.float32
        )
        chosen = live_rows & (band_of == index_band)
        summed = summed + jnp.where(chosen[None, :, :, None, None, None], partial_value, 0.0)
    return summed.reshape(field.shape).astype(jnp.bfloat16)


def to_bands(values):
    return lax.all_to_all(values, "wave", split_axis=2, concat_axis=1, tiled=True)


def shards_plain(control, wave_of_slot, legendre, vertical, points, lat_band, grid_scale, obs_weight):
    members, slots, rows_dev = (control.shape[0], control.shape[1], control.shape[2])
    slot_start = lax.axis_index("wave") * slots
    row_start = lax.axis_index("lev") * rows_dev
    own_waves = lax.dynamic_slice_in_dim(wave_of_slot, slot_start, slots)
    row_index = row_start + jnp.arange(rows_dev, dtype=jnp.int32)
    totals_n = own_waves[:, None] + row_index[None, :]
    live_rows = totals_n <= WAVES - 1
    band_of = jnp.minimum(totals_n * COV_BANDS // WAVES, COV_BANDS - 1)
    spectral = vertical_apply(control, vertical, live_rows, band_of, True)
    columns = lax.all_to_all(spectral, "lev", split_axis=4, concat_axis=2, tiled=True)
    col_dev = columns.shape[4]
    width = 2 * col_dev
    all_rows = columns.shape[2]
    columns = columns.reshape(members, slots, all_rows, width)
    coeffs = jnp.einsum(
        "skt,eskq->estq",
        lax.all_gather(legendre, "lev", axis=1, tiled=True),
        columns,
        preferred_element_type=jnp.float32,
    )
    coeffs = coeffs.astype(jnp.bfloat16)
    by_lat = to_bands(coeffs)
    wave_count = by_lat.shape[1]
    lat_dev = by_lat.shape[2]
    by_lat = by_lat.reshape(members, wave_count, lat_dev, 2, col_dev)
    fourier = fourier_table(wave_of_slot, points)
    synthesis = jnp.einsum("tspj,estpc->etcj", fourier, by_lat, preferred_element_type=jnp.float32)
    chooser = (
        lat_band[:, None] == jnp.arange(grid_scale.shape[0], dtype=jnp.int32)[None, :]
    ).astype(jnp.float32)
    lat_scale = jnp.dot(chooser, grid_scale, precision=lax.Precision.HIGHEST)
    increment = (synthesis * lat_scale[None, :, :, None]).astype(jnp.bfloat16)
    weighted = (
        increment.astype(jnp.float32) * obs_weight.astype(jnp.float32) * lat_scale[None, :, :, None]
    ).astype(jnp.bfloat16)
    adjoint_fourier = jnp.einsum(
        "tspj,etcj->etspc", fourier, weighted, preferred_element_type=jnp.float32
    )
    adjoint_fourier = adjoint_fourier.astype(jnp.bfloat16).reshape(
        members, lat_dev, wave_count, width
    )
    band_rows = to_bands(adjoint_fourier)
    adjoint_coeffs = jnp.einsum(
        "skt,etsq->eskq",
        lax.all_gather(legendre, "lev", axis=1, tiled=True),
        band_rows,
        preferred_element_type=jnp.float32,
    )
    adjoint_coeffs = adjoint_coeffs.astype(jnp.bfloat16).reshape(
        members, slots, all_rows, 2, col_dev
    )
    rows_back = lax.all_to_all(adjoint_coeffs, "lev", split_axis=2, concat_axis=4, tiled=True)
    gradient = vertical_apply(rows_back, vertical, live_rows, band_of, False)
    return (increment, gradient)


MESH = pl.DeviceIdType.MESH
VMEM_BYTES = 65000 * 1024
GROUPS = 2
RING = 4


def enter(n_wave, n_lev):
    me_w, me_l = lax.axis_index("wave"), lax.axis_index("lev")
    barrier = pltpu.get_barrier_semaphore()

    def greet(d, carry):
        peer = lax.rem(me_w + d, n_wave)
        pl.semaphore_signal(barrier, inc=1, device_id=(peer, me_l), device_id_type=MESH)
        return carry

    lax.fori_loop(1, n_wave, greet, 0)
    for d in range(1, n_lev):
        peer = lax.rem(me_l + d, n_lev)
        pl.semaphore_signal(barrier, inc=1, device_id=(me_w, peer), device_id_type=MESH)
    pl.semaphore_wait(barrier, n_wave + n_lev - 2)


def band_masks(total, waves):
    width = waves // COV_BANDS
    masks = []
    for b in range(COV_BANDS):
        hit = (total >= b * width) & (total < (b + 1) * width)
        masks.append(jnp.where(hit, 1.0, 0.0).astype(jnp.bfloat16))
    return masks


def banded_dot(x, masks, matrix):
    stacked = jnp.concatenate([x * mask for mask in masks], axis=1)
    return jnp.dot(stacked, matrix, preferred_element_type=jnp.float32)


SIN_TERMS = [(-1.0) ** i * (2.0 * math.pi) ** (2 * i + 1) / math.factorial(2 * i + 1) for i in range(10)]
COS_TERMS = [(-1.0) ** i * (2.0 * math.pi) ** (2 * i) / math.factorial(2 * i) for i in range(10)]


def horner(terms, square):
    value = jnp.full_like(square, terms[-1])
    for term in terms[-2::-1]:
        value = value * square + term
    return value


def loop(first, last, body):
    def step(i, carry):
        body(i)
        return carry

    lax.fori_loop(first, last, step, 0)


def transform_kernel(n_wave, n_lev, waves_ref, points_ref, order_ref, scale_ref, vf_ref, vg_ref, x_ref, l_ref, weight_ref,
                     inc_ref, grad_ref,
                     full, pieces, own, away, spec, back, flat, wsend, land, aland, table, wbuf, ibuf, stage,
                     full_sem, x_sem, weight_sem, inc_sem, grad_sem, l_send, l_recv, f_send, f_recv, b_send, b_recv,
                     w_send, w_recv, a_send, a_recv):
    members, slots, rows = x_ref.shape[:3]
    per = vf_ref.shape[0] // n_lev
    lats, cols, longs = weight_ref.shape
    waves = n_wave * slots
    lat_all = n_wave * lats
    chunks = members * per
    size = slots // GROUPS
    units = chunks * GROUPS
    me_w, me_l = lax.axis_index("wave"), lax.axis_index("lev")
    row0 = me_l * rows
    bf16, f32 = jnp.bfloat16, jnp.float32

    def where_is(u):
        q, g = lax.div(u, GROUPS), lax.rem(u, GROUPS)
        return q, g, lax.div(q, per), lax.rem(q, per)

    def level_block(d, i):
        a = lax.rem(me_l + d, n_lev) * per + i
        return a, pl.ds(pl.multiple_of(a * LEVELS, LEVELS), LEVELS)

    def group_slots(g):
        return pl.ds(pl.multiple_of(g * size, size), size)

    def x_copy(u, d):
        _, g, e, i = where_is(u)
        slot = lax.rem(u, 2)
        return pltpu.make_async_copy(
            x_ref.at[e, group_slots(g), :, :, level_block(d, i)[1]], pieces.at[slot, d], x_sem.at[slot, d])

    def grad_copy(u, d):
        _, g, e, i = where_is(u)
        slot = lax.rem(u, 2)
        return pltpu.make_async_copy(
            pieces.at[slot, d], grad_ref.at[e, group_slots(g), :, :, level_block(d, i)[1]], grad_sem.at[slot, d])

    def weight_copy(q):
        i = lax.rem(q, per)
        return pltpu.make_async_copy(
            weight_ref.at[:, pl.ds(pl.multiple_of(i * LEVELS, LEVELS), LEVELS), :], wbuf, weight_sem)

    def inc_copy(q):
        e, i = lax.div(q, per), lax.rem(q, per)
        return pltpu.make_async_copy(
            ibuf, inc_ref.at[e, :, pl.ds(pl.multiple_of(i * LEVELS, LEVELS), LEVELS), :], inc_sem)

    def full_copy():
        return pltpu.make_async_copy(l_ref, full.at[me_l], full_sem)

    def table_copy(g, d):
        peer = lax.rem(me_l + d, n_lev)
        return pltpu.make_async_remote_copy(
            src_ref=l_ref.at[group_slots(g)], dst_ref=full.at[me_l, group_slots(g)],
            send_sem=l_send.at[g, d - 1], recv_sem=l_recv.at[g, d - 1],
            device_id=(me_w, peer), device_id_type=MESH)

    def lev_copy(u, d, target, send_sem, recv_sem):
        peer = lax.rem(me_l + d, n_lev)
        return pltpu.make_async_remote_copy(
            src_ref=away.at[lax.rem(u, RING), d - 1], dst_ref=target.at[u, n_lev - d - 1],
            send_sem=send_sem.at[u, d - 1], recv_sem=recv_sem.at[u, d - 1],
            device_id=(me_w, peer), device_id_type=MESH)

    def out_copy(u, d):
        return lev_copy(u, d, spec, f_send, f_recv)

    def back_copy(u, d):
        return lev_copy(u, d, back, b_send, b_recv)

    def wave_copy(u, d, target, send_sem, recv_sem):
        peer = lax.rem(me_w + d, n_wave)
        return pltpu.make_async_remote_copy(
            src_ref=wsend.at[u, peer], dst_ref=target.at[u, me_w],
            send_sem=send_sem.at[u, d - 1], recv_sem=recv_sem.at[u, d - 1],
            device_id=(peer, me_l), device_id_type=MESH)

    def land_copy(u, d):
        return wave_copy(u, d, land, w_send, w_recv)

    def aland_copy(u, d):
        return wave_copy(u, d, aland, a_send, a_recv)

    lev_others = range(1, n_lev)
    lev_order = list(lev_others) + [0]

    def vertical(u):
        _, g, e, i = where_is(u)
        slot, keep = lax.rem(u, 2), lax.rem(u, RING)
        for d in range(n_lev):
            x_copy(u, d).wait()

        @pl.when(u >= RING)
        def _():
            for d in lev_others:
                out_copy(u - RING, d).wait_send()

        def one(s):
            wave = waves_ref[g * size + s]
            total = wave + row0 + lax.div(lax.broadcasted_iota(jnp.int32, (2 * rows, LEVELS), 0), 2)
            masks = band_masks(total, waves)
            for d in lev_order:
                a, _ = level_block(d, i)
                x = pieces.at[slot, d].reshape(size, 2 * rows, LEVELS)[s]
                stage[d] = banded_dot(x, masks, vf_ref[a])
                for p in range(2):
                    y = stage[d, pl.ds(p, rows, stride=2), :].astype(bf16)
                    if d == 0:
                        own[keep, s, :, p * LEVELS:(p + 1) * LEVELS] = y
                    else:
                        away[keep, d - 1, s, :, p * LEVELS:(p + 1) * LEVELS] = y

        loop(0, size, one)
        for d in lev_others:
            out_copy(u, d).start()

        @pl.when(u + 2 < units)
        def _():
            for d in range(n_lev):
                x_copy(u + 2, d).start()

        @pl.when(u + 1 < GROUPS)
        def _():
            for d in lev_others:
                table_copy(u + 1, d).start()

    def legendre(u):
        _, g, e, i = where_is(u)
        keep = lax.rem(u, RING)
        coef = flat.reshape(size, lat_all, 2 * LEVELS)

        @pl.when(u == 0)
        def _():
            full_copy().wait()

        @pl.when(u < GROUPS)
        def _():
            for d in lev_others:
                table_copy(u, d).wait()

        for d in lev_others:
            out_copy(u, d).wait_recv()

        def one(s):
            fields, tables = [], []
            for d in range(n_lev):
                fields.append(own[keep, s] if d == 0 else spec[u, d - 1, s])
                tables.append(full[lax.rem(me_l + d, n_lev), g * size + s])
            coef[s] = lax.dot_general(
                jnp.concatenate(tables, axis=0), jnp.concatenate(fields, axis=0),
                (((0,), (0,)), ((), ())), preferred_element_type=f32)

        loop(0, size, one)

        def turn(w):
            for t in range(lats):
                wsend[u, w, t] = coef[:, w * lats + t, :].astype(bf16)

        loop(0, n_wave, turn)
        loop(1, n_wave, lambda d: land_copy(u, d).start())
        land[u, me_w] = wsend[u, me_w]

    def build(t):
        points = points_ref[t]
        n = points.astype(f32)
        piece = 32
        inverse = 1.0 / jnp.full((1, longs), n, f32)
        lane = lax.broadcasted_iota(jnp.int32, (1, longs), 1)
        inside = jnp.where(lane < points, 1.0, 0.0) / math.sqrt(4.0 * waves)

        def some(k):
            base = pl.multiple_of(k * piece, piece)
            wave = order_ref[pl.ds(base, piece), :]
            product = wave * lane.astype(f32)
            turns = jnp.floor(product * inverse + 0.5)
            x = (product - turns * n) * inverse
            square = x * x
            gain = jnp.where(wave == 0.0, 1.0, 2.0) * inside
            table[t, pl.ds(base, piece), :] = (gain * horner(COS_TERMS, square)).astype(bf16)
            sine = (-gain) * (x * horner(SIN_TERMS, square))
            table[t, pl.ds(pl.multiple_of(waves + base, piece), piece), :] = sine.astype(bf16)

        loop(0, waves // piece, some)

    def grid(q):
        i = lax.rem(q, per)
        weight_copy(q).wait()

        @pl.when(q > 0)
        def _():
            inc_copy(q - 1).wait()

        for g in range(GROUPS):
            loop(1, n_wave, lambda d: land_copy(q * GROUPS + g, d).wait())
        here = pl.ds(q * GROUPS, GROUPS)
        scales = scale_ref[pl.ds(pl.multiple_of(i * LEVELS, LEVELS), LEVELS), :]
        column = lax.broadcasted_iota(jnp.int32, scales.shape, 1)

        def one(t):
            scale = jnp.sum(jnp.where(column == t, scales, 0.0), axis=1, keepdims=True)
            parts = [land[here, :, t, :, p * LEVELS:(p + 1) * LEVELS].reshape(waves, LEVELS) for p in range(2)]
            synthesis = lax.dot_general(jnp.concatenate(parts, axis=0), table[t], (((0,), (0,)), ((), ())),
                                        preferred_element_type=f32)
            increment = (synthesis * scale).astype(bf16)
            ibuf[t] = increment
            weighted = increment.astype(f32) * wbuf[t].astype(f32) * scale
            adjoint = lax.dot_general(table[t], weighted.astype(bf16), (((1,), (1,)), ((), ())),
                                      preferred_element_type=f32).astype(bf16)
            for p in range(2):
                part = adjoint[p * waves:(p + 1) * waves].reshape(GROUPS, n_wave, size, LEVELS)
                wsend[here, :, t, :, p * LEVELS:(p + 1) * LEVELS] = part

        loop(0, lats, one)
        for g in range(GROUPS):
            u = q * GROUPS + g
            loop(1, n_wave, lambda d: aland_copy(u, d).start())
            aland[u, me_w] = wsend[u, me_w]
        inc_copy(q).start()

        @pl.when(q + 1 < chunks)
        def _():
            weight_copy(q + 1).start()

    def adjoint_legendre(u):
        _, g, e, i = where_is(u)
        keep = lax.rem(u, RING)
        fine = flat.reshape(lat_all, size, 2 * LEVELS)
        loop(1, n_wave, lambda d: aland_copy(u, d).wait())

        @pl.when(u < RING)
        def _():
            for d in lev_others:
                out_copy(u + units - RING, d).wait_send()

        @pl.when(u >= RING)
        def _():
            for d in lev_others:
                back_copy(u - RING, d).wait_send()

        def widen(w):
            fine[pl.ds(pl.multiple_of(w * lats, lats), lats)] = aland[u, w].astype(f32)

        loop(0, n_wave, widen)

        def one(s):
            field = fine[:, s, :].astype(bf16)
            for d in lev_order:
                y = jnp.dot(full[lax.rem(me_l + d, n_lev), g * size + s], field, preferred_element_type=f32).astype(bf16)
                if d == 0:
                    own[keep, s] = y
                else:
                    away[keep, d - 1, s] = y

        loop(0, size, one)
        for d in lev_others:
            back_copy(u, d).start()

    def adjoint_vertical(u):
        _, g, e, i = where_is(u)
        slot, keep = lax.rem(u, 2), lax.rem(u, RING)
        for d in lev_others:
            back_copy(u, d).wait_recv()

        @pl.when(u >= 2)
        def _():
            for d in range(n_lev):
                grad_copy(u - 2, d).wait()

        def one(s):
            wave = waves_ref[g * size + s]
            masks = band_masks(wave + row0 + lax.broadcasted_iota(jnp.int32, (rows, LEVELS), 0), waves)
            for d in range(n_lev):
                a, _ = level_block(d, i)
                for p in range(2):
                    at = slice(p * LEVELS, (p + 1) * LEVELS)
                    x = own[keep, s, :, at] if d == 0 else back[u, d - 1, s, :, at]
                    stage[d, pl.ds(p, rows, stride=2), :] = banded_dot(x, masks, vg_ref[a])
                pieces.at[slot, d].reshape(size, 2 * rows, LEVELS)[s] = stage[d].astype(bf16)

        loop(0, size, one)
        for d in range(n_lev):
            grad_copy(u, d).start()

    ahead = RING - 1
    full_copy().start()
    for u in range(2):
        for d in range(n_lev):
            x_copy(u, d).start()
    weight_copy(0).start()
    enter(n_wave, n_lev)
    for d in lev_others:
        table_copy(0, d).start()
    loop(0, ahead, vertical)
    loop(0, lats // 2, build)

    def front(u):
        legendre(u)
        vertical(u + ahead)

        @pl.when(u == 0)
        def _():
            loop(lats // 2, lats, build)

    loop(0, units - ahead, front)
    loop(units - ahead, units, legendre)
    loop(0, chunks, grid)
    adjoint_legendre(0)

    def tail(u):
        adjoint_legendre(u + 1)
        adjoint_vertical(u)

    loop(0, units - 1, tail)
    adjoint_vertical(units - 1)
    inc_copy(chunks - 1).wait()
    for u in range(units - 2, units):
        for d in range(n_lev):
            grad_copy(u, d).wait()
    for u in range(units - RING, units):
        for d in lev_others:
            back_copy(u, d).wait_send()


def shards_kernel(n_wave, n_lev, control, wave_of_slot, legendre, vertical, points, lat_band, grid_scale, obs_weight):
    members, slots, rows = control.shape[:3]
    waves = wave_of_slot.shape[0]
    variables = vertical.shape[1]
    columns = control.shape[4]
    cols = columns // n_lev
    lats, _, longs = obs_weight.shape
    per = variables // n_lev
    chunks = members * per
    size = slots // GROUPS
    units = chunks * GROUPS
    bf16, f32 = jnp.bfloat16, jnp.float32
    own_waves = lax.dynamic_slice_in_dim(wave_of_slot, lax.axis_index("wave") * slots, slots)
    order = wave_of_slot.reshape(n_wave, GROUPS, size).transpose(1, 0, 2).reshape(waves, 1).astype(f32)
    stack_f = vertical.transpose(1, 0, 3, 2).reshape(variables, COV_BANDS * LEVELS, LEVELS)
    stack_g = vertical.transpose(1, 0, 2, 3).reshape(variables, COV_BANDS * LEVELS, LEVELS)
    chooser = (
        lat_band[:, None] == jnp.arange(grid_scale.shape[0], dtype=jnp.int32)[None, :]
    ).astype(f32)
    lat_scale = jnp.dot(chooser, grid_scale, precision=lax.Precision.HIGHEST).T
    vmem = pl.BlockSpec(memory_space=pltpu.VMEM)
    smem = pl.BlockSpec(memory_space=pltpu.SMEM)
    hbm = pl.BlockSpec(memory_space=pl.ANY)
    dma = pltpu.SemaphoreType.DMA
    others = n_lev - 1
    half = (size, rows, 2 * LEVELS)
    packet = (units, n_wave, lats, size, 2 * LEVELS)
    return pl.pallas_call(
        functools.partial(transform_kernel, n_wave, n_lev),
        out_shape=[
            jax.ShapeDtypeStruct((members, lats, cols, longs), bf16),
            jax.ShapeDtypeStruct(control.shape, bf16),
        ],
        in_specs=[smem, smem, vmem, vmem, vmem, vmem, hbm, hbm, hbm],
        out_specs=[hbm, hbm],
        scratch_shapes=[
            pltpu.VMEM((n_lev, *legendre.shape), bf16),
            pltpu.VMEM((2, n_lev, size, rows, 2, LEVELS), bf16),
            pltpu.VMEM((RING, *half), bf16),
            pltpu.VMEM((RING, others, *half), bf16),
            pltpu.VMEM((units, others, *half), bf16),
            pltpu.VMEM((units, others, *half), bf16),
            pltpu.VMEM((size * n_wave * lats, 2 * LEVELS), f32),
            pltpu.VMEM(packet, bf16),
            pltpu.VMEM(packet, bf16),
            pltpu.VMEM(packet, bf16),
            pltpu.VMEM((lats, 2 * waves, longs), bf16),
            pltpu.VMEM((lats, LEVELS, longs), bf16),
            pltpu.VMEM((lats, LEVELS, longs), bf16),
            pltpu.VMEM((n_lev, 2 * rows, LEVELS), f32),
            dma, dma((2, n_lev)), dma, dma, dma((2, n_lev)),
            dma((GROUPS, others)), dma((GROUPS, others)),
            dma((units, others)), dma((units, others)), dma((units, others)), dma((units, others)),
            dma((units, n_wave - 1)), dma((units, n_wave - 1)), dma((units, n_wave - 1)), dma((units, n_wave - 1)),
        ],
        compiler_params=pltpu.CompilerParams(collective_id=0, has_side_effects=True, vmem_limit_bytes=VMEM_BYTES),
        name="transform",
    )(own_waves, points, order, lat_scale, stack_f, stack_g, control, legendre, obs_weight)


def shards(n_wave, n_lev, *arrays):
    slots, rows, columns = arrays[0].shape[1], arrays[0].shape[2], arrays[0].shape[4]
    whole_tiles = slots % 16 == 0 and rows % 128 == 0 and columns % (n_lev * LEVELS) == 0
    if whole_tiles and n_lev > 1:
        return shards_kernel(n_wave, n_lev, *arrays)
    return shards_plain(*arrays)


def solution(mesh):
    in_specs = (
        P(None, "wave", "lev", None, None),
        P(),
        P("wave", "lev", None),
        P(),
        P("wave"),
        P("wave"),
        P(None, "lev"),
        P("wave", "lev", None),
    )
    out_specs = (P(None, "wave", "lev", None), P(None, "wave", "lev", None, None))
    body = functools.partial(shards, mesh.shape["wave"], mesh.shape["lev"])
    return jax.shard_map(body, mesh=mesh, in_specs=in_specs, out_specs=out_specs, check_vma=False)
```

time: 556 us -> 451 us (0.81)
  Pallas kernels: 517 us -> 426 us
  local copies, waits for them, and re-layouts: 38.1 us -> 21.8 us
    pallas_call x3 -> x1, Pallas kernels: 517 us -> 426 us  [shards_kernel(): pl.pallas_call(functools.partial(transform_kernel, n_wave, n_lev), out_sh...]
    reshape x1 -> x0, local copies, waits for them, and re-layouts: 16.4 us -> none  [shards_kernels(): gradient.reshape(members, 2, slots, rows, columns).transpose(0, 2, 3, 1, 4)]
    transpose x3 -> x2, local copies, waits for them, and re-layouts: 10.6 us -> 3.92 us  [the longest x1 2.04 us: shards_kernel(): vertical.transpose(1, 0, 3, 2)]
    unnamed x18 -> x4, local copies, waits for them, and re-layouts: 8.99 us -> 15.7 us
where the time goes in v1:
time: 451 us; the launch traced here: 450 us
  Pallas kernels  426 us (94%)
  local copies, waits for them, and re-layouts  21.8 us (5%)
    pallas_call x1, Pallas kernels, shards_kernel(): pl.pallas_call(functools.partial(transform_kernel, n_wave, n_lev), out_sh...  426 us
    unnamed x4, local copies, waits for them, and re-layouts  15.7 us

profile of v1, /device:TPU:29, one launch (start us, length us, event | category | flops | bytes accessed | tf_op | source)
XLA Modules:
  0.0 450.3 jit_solution(11730011738233340858)
XLA Ops:
  0.6 0.0 copy-start
  0.6 1.3 dynamic_slice.3.waves_ref
  2.0 0.7 convert_element_type.10
  2.7 0.1 convert_element_type.11
  2.8 0.7 convert_element_type.14.order_ref
  3.5 0.0 copy-done
  3.5 1.6 convolution_bitcast_fusion.scale_ref
  5.1 2.0 copy.15
  7.2 1.9 copy.16
  9.1 425.6 %transform.1 = (bf16[2,16,256,512]{3,2,1,0:T(8,128)(2,1)}, bf16[2,16,128,2,512]{4,3,2,1,0:T(2,128)(2,1)}) custom-call(s32[16]{0:T(128)} %dynamic_slice.3.waves_ref, s32[16]{0:T(128)} %points_ref.1, f32[256,1]{1,0:T(8,128)} %convert_element_type.14.order_ref, f32[256,16]{1,0:T(8,128)} %convolution_bitcast_fusion.scale_ref, bf16[4,512,128]{2,1,0:T(8,128)(2,1)} %bitcast.10, ...), custom_call_target="tpu_custom_call" | custom-call | tf_op jit(solution)/shard_map/transform/pallas_call | solution.py:517
  434.6 7.7 %copy.21 = bf16[2,16,256,512]{3,2,1,0:T(8,128)(2,1)} copy(bf16[2,16,256,512]{3,2,1,0:T(8,128)(2,1)} %get-tuple-element.4) | data formatting | bytes 16777216
  442.3 8.0 %copy.22 = bf16[2,16,128,2,512]{4,3,2,1,0:T(2,128)(2,1)} copy(bf16[2,16,128,2,512]{4,3,2,1,0:T(2,128)(2,1)} %get-tuple-element.5) | data formatting | bytes 16777216
  (1 shorter events, 0.0 us)
Async XLA Ops:
  0.6 2.9 copy-start

commit v2 on v1

--- a/solution.py
+++ b/solution.py
@@ -108,24 +108,26 @@
 
 MESH = pl.DeviceIdType.MESH
 VMEM_BYTES = 65000 * 1024
-GROUPS = 2
-RING = 4
-
-
-def enter(n_wave, n_lev):
+PAIR = 2
+RING = 8
+AHEAD = 4
+PIECES = 4
+
+
+def greet(n_wave, n_lev):
     me_w, me_l = lax.axis_index("wave"), lax.axis_index("lev")
     barrier = pltpu.get_barrier_semaphore()
 
-    def greet(d, carry):
+    def one(d, carry):
         peer = lax.rem(me_w + d, n_wave)
         pl.semaphore_signal(barrier, inc=1, device_id=(peer, me_l), device_id_type=MESH)
         return carry
 
-    lax.fori_loop(1, n_wave, greet, 0)
+    lax.fori_loop(1, n_wave, one, 0)
     for d in range(1, n_lev):
         peer = lax.rem(me_l + d, n_lev)
         pl.semaphore_signal(barrier, inc=1, device_id=(me_w, peer), device_id_type=MESH)
-    pl.semaphore_wait(barrier, n_wave + n_lev - 2)
+    return barrier
 
 
 def band_masks(total, waves):
@@ -161,45 +163,46 @@
     lax.fori_loop(first, last, step, 0)
 
 
-def transform_kernel(n_wave, n_lev, waves_ref, points_ref, order_ref, scale_ref, vf_ref, vg_ref, x_ref, l_ref, weight_ref,
+def transform_kernel(n_wave, n_lev, waves_ref, points_ref, band_ref, grid_scale_ref, v_ref, x_ref, l_ref, weight_ref,
                      inc_ref, grad_ref,
-                     full, pieces, own, away, spec, back, flat, wsend, land, aland, table, wbuf, ibuf, stage,
-                     full_sem, x_sem, weight_sem, inc_sem, grad_sem, l_send, l_recv, f_send, f_recv, b_send, b_recv,
+                     full, mats, mats_t, order, pieces, own, away, spec, back, coef, wsend, asend, land, aland, table, wbuf, ibuf, stage,
+                     full_sem, mats_sem, x_sem, weight_sem, inc_sem, grad_sem, l_send, l_recv, f_send, f_recv, b_send, b_recv,
                      w_send, w_recv, a_send, a_recv):
     members, slots, rows = x_ref.shape[:3]
-    per = vf_ref.shape[0] // n_lev
+    variables = v_ref.shape[1]
+    per = variables // n_lev
     lats, cols, longs = weight_ref.shape
     waves = n_wave * slots
     lat_all = n_wave * lats
     chunks = members * per
-    size = slots // GROUPS
-    units = chunks * GROUPS
+    subs = slots // PAIR
+    units = chunks * subs
     me_w, me_l = lax.axis_index("wave"), lax.axis_index("lev")
     row0 = me_l * rows
     bf16, f32 = jnp.bfloat16, jnp.float32
 
     def where_is(u):
-        q, g = lax.div(u, GROUPS), lax.rem(u, GROUPS)
+        q, g = lax.div(u, subs), lax.rem(u, subs)
         return q, g, lax.div(q, per), lax.rem(q, per)
 
     def level_block(d, i):
         a = lax.rem(me_l + d, n_lev) * per + i
         return a, pl.ds(pl.multiple_of(a * LEVELS, LEVELS), LEVELS)
 
-    def group_slots(g):
-        return pl.ds(pl.multiple_of(g * size, size), size)
+    def pair_slots(g):
+        return pl.ds(g * PAIR, PAIR)
 
     def x_copy(u, d):
         _, g, e, i = where_is(u)
-        slot = lax.rem(u, 2)
+        slot = lax.rem(u, PIECES)
         return pltpu.make_async_copy(
-            x_ref.at[e, group_slots(g), :, :, level_block(d, i)[1]], pieces.at[slot, d], x_sem.at[slot, d])
+            x_ref.at[e, pair_slots(g), :, :, level_block(d, i)[1]], pieces.at[slot, d], x_sem.at[slot, d])
 
     def grad_copy(u, d):
         _, g, e, i = where_is(u)
-        slot = lax.rem(u, 2)
+        slot = lax.rem(u, PIECES)
         return pltpu.make_async_copy(
-            pieces.at[slot, d], grad_ref.at[e, group_slots(g), :, :, level_block(d, i)[1]], grad_sem.at[slot, d])
+            pieces.at[slot, d], grad_ref.at[e, pair_slots(g), :, :, level_block(d, i)[1]], grad_sem.at[slot, d])
 
     def weight_copy(q):
         i = lax.rem(q, per)
@@ -214,10 +217,13 @@
     def full_copy():
         return pltpu.make_async_copy(l_ref, full.at[me_l], full_sem)
 
+    def mats_copy():
+        return pltpu.make_async_copy(v_ref, mats, mats_sem)
+
     def table_copy(g, d):
         peer = lax.rem(me_l + d, n_lev)
         return pltpu.make_async_remote_copy(
-            src_ref=l_ref.at[group_slots(g)], dst_ref=full.at[me_l, group_slots(g)],
+            src_ref=l_ref.at[pair_slots(g)], dst_ref=full.at[me_l, pair_slots(g)],
             send_sem=l_send.at[g, d - 1], recv_sem=l_recv.at[g, d - 1],
             device_id=(me_w, peer), device_id_type=MESH)
 
@@ -234,25 +240,40 @@
     def back_copy(u, d):
         return lev_copy(u, d, back, b_send, b_recv)
 
-    def wave_copy(u, d, target, send_sem, recv_sem):
+    def remote(src, dst, send_sem, recv_sem, d):
+        return pltpu.make_async_remote_copy(
+            src_ref=src, dst_ref=dst, send_sem=send_sem, recv_sem=recv_sem,
+            device_id=(lax.rem(me_w + d, n_wave), me_l), device_id_type=MESH)
+
+    def land_copy(u, d):
+        q, g, _, _ = where_is(u)
         peer = lax.rem(me_w + d, n_wave)
-        return pltpu.make_async_remote_copy(
-            src_ref=wsend.at[u, peer], dst_ref=target.at[u, me_w],
-            send_sem=send_sem.at[u, d - 1], recv_sem=recv_sem.at[u, d - 1],
-            device_id=(peer, me_l), device_id_type=MESH)
-
-    def land_copy(u, d):
-        return wave_copy(u, d, land, w_send, w_recv)
+        return remote(wsend.at[q, g, :, peer], land.at[q, :, :, g, me_w], w_send.at[u], w_recv.at[u], d)
+
+    def land_all(u):
+        q, g, _, _ = where_is(u)
+        most = pl.ds(0, n_wave - 1)
+        return remote(wsend.at[q, g, :, most], land.at[q, :, :, g, most], w_send.at[u], w_recv.at[u], 1)
 
     def aland_copy(u, d):
-        return wave_copy(u, d, aland, a_send, a_recv)
+        q, g, _, _ = where_is(u)
+        peer = lax.rem(me_w + d, n_wave)
+        return remote(asend.at[q, :, :, g, peer], aland.at[u, :, me_w], a_send.at[u], a_recv.at[u], d)
+
+    def aland_all(u):
+        q, g, _, _ = where_is(u)
+        most = pl.ds(0, n_wave - 1)
+        return remote(asend.at[q, :, :, g, most], aland.at[u, :, most], a_send.at[u], a_recv.at[u], 1)
 
     lev_others = range(1, n_lev)
     lev_order = list(lev_others) + [0]
 
+    def own_wave(g, s):
+        return waves_ref[me_w * slots + g * PAIR + s]
+
     def vertical(u):
         _, g, e, i = where_is(u)
-        slot, keep = lax.rem(u, 2), lax.rem(u, RING)
+        slot, keep = lax.rem(u, PIECES), lax.rem(u, RING)
         for d in range(n_lev):
             x_copy(u, d).wait()
 
@@ -261,45 +282,43 @@
             for d in lev_others:
                 out_copy(u - RING, d).wait_send()
 
-        def one(s):
-            wave = waves_ref[g * size + s]
-            total = wave + row0 + lax.div(lax.broadcasted_iota(jnp.int32, (2 * rows, LEVELS), 0), 2)
+        for s in range(PAIR):
+            total = own_wave(g, s) + row0 + lax.div(lax.broadcasted_iota(jnp.int32, (2 * rows, LEVELS), 0), 2)
             masks = band_masks(total, waves)
             for d in lev_order:
                 a, _ = level_block(d, i)
-                x = pieces.at[slot, d].reshape(size, 2 * rows, LEVELS)[s]
-                stage[d] = banded_dot(x, masks, vf_ref[a])
+                x = pieces.at[slot, d].reshape(PAIR, 2 * rows, LEVELS)[s]
+                stage[s, d] = banded_dot(x, masks, mats_t[a])
                 for p in range(2):
-                    y = stage[d, pl.ds(p, rows, stride=2), :].astype(bf16)
+                    y = stage[s, d, pl.ds(p, rows, stride=2), :].astype(bf16)
                     if d == 0:
                         own[keep, s, :, p * LEVELS:(p + 1) * LEVELS] = y
                     else:
                         away[keep, d - 1, s, :, p * LEVELS:(p + 1) * LEVELS] = y
 
-        loop(0, size, one)
+        @pl.when(u + PIECES < units)
+        def _():
+            for d in range(n_lev):
+                x_copy(u + PIECES, d).start()
+
+    def send_levels(u):
         for d in lev_others:
             out_copy(u, d).start()
 
-        @pl.when(u + 2 < units)
-        def _():
-            for d in range(n_lev):
-                x_copy(u + 2, d).start()
-
-        @pl.when(u + 1 < GROUPS)
+        @pl.when(u + 1 < subs)
         def _():
             for d in lev_others:
                 table_copy(u + 1, d).start()
 
     def legendre(u):
-        _, g, e, i = where_is(u)
+        q, g, e, i = where_is(u)
         keep = lax.rem(u, RING)
-        coef = flat.reshape(size, lat_all, 2 * LEVELS)
 
         @pl.when(u == 0)
         def _():
             full_copy().wait()
 
-        @pl.when(u < GROUPS)
+        @pl.when(u < subs)
         def _():
             for d in lev_others:
                 table_copy(u, d).wait()
@@ -307,24 +326,32 @@
         for d in lev_others:
             out_copy(u, d).wait_recv()
 
-        def one(s):
+        for s in range(PAIR):
             fields, tables = [], []
             for d in range(n_lev):
                 fields.append(own[keep, s] if d == 0 else spec[u, d - 1, s])
-                tables.append(full[lax.rem(me_l + d, n_lev), g * size + s])
-            coef[s] = lax.dot_general(
+                tables.append(full[lax.rem(me_l + d, n_lev), g * PAIR + s])
+            value = lax.dot_general(
                 jnp.concatenate(tables, axis=0), jnp.concatenate(fields, axis=0),
                 (((0,), (0,)), ((), ())), preferred_element_type=f32)
-
-        loop(0, size, one)
-
-        def turn(w):
-            for t in range(lats):
-                wsend[u, w, t] = coef[:, w * lats + t, :].astype(bf16)
-
-        loop(0, n_wave, turn)
+            for p in range(2):
+                coef[p, pl.ds(s, lat_all, stride=PAIR), :] = value[:, p * LEVELS:(p + 1) * LEVELS]
+        for p in range(2):
+            wsend.at[q, g, p].reshape(lat_all * PAIR, LEVELS)[...] = coef[p].astype(bf16)
         loop(1, n_wave, lambda d: land_copy(u, d).start())
-        land[u, me_w] = wsend[u, me_w]
+        land[q, :, :, g, me_w] = wsend[q, g, :, me_w]
+
+    def make_order():
+        def some(k):
+            row = lax.broadcasted_iota(jnp.int32, (8, LEVELS), 0)
+            values = jnp.zeros((8, LEVELS), jnp.int32)
+            for j in range(8):
+                r = k * 8 + j
+                g, w, s = lax.div(r, n_wave * PAIR), lax.rem(lax.div(r, PAIR), n_wave), lax.rem(r, PAIR)
+                values = jnp.where(row == j, waves_ref[w * slots + g * PAIR + s], values)
+            order[pl.ds(pl.multiple_of(k * 8, 8), 8), :] = values.astype(f32)
+
+        loop(0, waves // 8, some)
 
     def build(t):
         points = points_ref[t]
@@ -336,7 +363,7 @@
 
         def some(k):
             base = pl.multiple_of(k * piece, piece)
-            wave = order_ref[pl.ds(base, piece), :]
+            wave = order[pl.ds(base, piece), 0:1]
             product = wave * lane.astype(f32)
             turns = jnp.floor(product * inverse + 0.5)
             x = (product - turns * n) * inverse
@@ -348,6 +375,14 @@
 
         loop(0, waves // piece, some)
 
+    def scale_column(t, i):
+        block = grid_scale_ref[:, pl.ds(pl.multiple_of(i * LEVELS, LEVELS), LEVELS)]
+        band = lax.broadcasted_iota(jnp.int32, block.shape, 0)
+        line = jnp.sum(jnp.where(band == band_ref[t], block, 0.0), axis=0, keepdims=True)
+        square = (LEVELS, LEVELS)
+        diagonal = lax.broadcasted_iota(jnp.int32, square, 0) == lax.broadcasted_iota(jnp.int32, square, 1)
+        return jnp.sum(jnp.where(diagonal, line, 0.0), axis=1, keepdims=True)
+
     def grid(q):
         i = lax.rem(q, per)
         weight_copy(q).wait()
@@ -356,15 +391,11 @@
         def _():
             inc_copy(q - 1).wait()
 
-        for g in range(GROUPS):
-            loop(1, n_wave, lambda d: land_copy(q * GROUPS + g, d).wait())
-        here = pl.ds(q * GROUPS, GROUPS)
-        scales = scale_ref[pl.ds(pl.multiple_of(i * LEVELS, LEVELS), LEVELS), :]
-        column = lax.broadcasted_iota(jnp.int32, scales.shape, 1)
+        loop(0, subs, lambda g: land_all(q * subs + g).wait())
 
         def one(t):
-            scale = jnp.sum(jnp.where(column == t, scales, 0.0), axis=1, keepdims=True)
-            parts = [land[here, :, t, :, p * LEVELS:(p + 1) * LEVELS].reshape(waves, LEVELS) for p in range(2)]
+            scale = scale_column(t, i)
+            parts = [land.at[q, p, t].reshape(waves, LEVELS)[...] for p in range(2)]
             synthesis = lax.dot_general(jnp.concatenate(parts, axis=0), table[t], (((0,), (0,)), ((), ())),
                                         preferred_element_type=f32)
             increment = (synthesis * scale).astype(bf16)
@@ -373,14 +404,16 @@
             adjoint = lax.dot_general(table[t], weighted.astype(bf16), (((1,), (1,)), ((), ())),
                                       preferred_element_type=f32).astype(bf16)
             for p in range(2):
-                part = adjoint[p * waves:(p + 1) * waves].reshape(GROUPS, n_wave, size, LEVELS)
-                wsend[here, :, t, :, p * LEVELS:(p + 1) * LEVELS] = part
+                asend.at[q, p, t].reshape(waves, LEVELS)[...] = adjoint[p * waves:(p + 1) * waves]
 
         loop(0, lats, one)
-        for g in range(GROUPS):
-            u = q * GROUPS + g
+
+        def send(g):
+            u = q * subs + g
             loop(1, n_wave, lambda d: aland_copy(u, d).start())
-            aland[u, me_w] = wsend[u, me_w]
+            aland[u, :, me_w] = asend[q, :, :, g, me_w]
+
+        loop(0, subs, send)
         inc_copy(q).start()
 
         @pl.when(q + 1 < chunks)
@@ -390,8 +423,7 @@
     def adjoint_legendre(u):
         _, g, e, i = where_is(u)
         keep = lax.rem(u, RING)
-        fine = flat.reshape(lat_all, size, 2 * LEVELS)
-        loop(1, n_wave, lambda d: aland_copy(u, d).wait())
+        aland_all(u).wait()
 
         @pl.when(u < RING)
         def _():
@@ -403,88 +435,102 @@
             for d in lev_others:
                 back_copy(u - RING, d).wait_send()
 
-        def widen(w):
-            fine[pl.ds(pl.multiple_of(w * lats, lats), lats)] = aland[u, w].astype(f32)
-
-        loop(0, n_wave, widen)
-
-        def one(s):
-            field = fine[:, s, :].astype(bf16)
+        for p in range(2):
+            coef[p] = aland.at[u, p].reshape(lat_all * PAIR, LEVELS)[...].astype(f32)
+        for s in range(PAIR):
+            field = jnp.concatenate(
+                [coef[p, pl.ds(s, lat_all, stride=PAIR), :].astype(bf16) for p in range(2)], axis=1)
             for d in lev_order:
-                y = jnp.dot(full[lax.rem(me_l + d, n_lev), g * size + s], field, preferred_element_type=f32).astype(bf16)
+                y = jnp.dot(full[lax.rem(me_l + d, n_lev), g * PAIR + s], field, preferred_element_type=f32).astype(bf16)
                 if d == 0:
                     own[keep, s] = y
                 else:
                     away[keep, d - 1, s] = y
-
-        loop(0, size, one)
         for d in lev_others:
             back_copy(u, d).start()
 
     def adjoint_vertical(u):
         _, g, e, i = where_is(u)
-        slot, keep = lax.rem(u, 2), lax.rem(u, RING)
+        slot, keep = lax.rem(u, PIECES), lax.rem(u, RING)
         for d in lev_others:
             back_copy(u, d).wait_recv()
 
-        @pl.when(u >= 2)
+        @pl.when(u >= PIECES)
         def _():
             for d in range(n_lev):
-                grad_copy(u - 2, d).wait()
-
-        def one(s):
-            wave = waves_ref[g * size + s]
-            masks = band_masks(wave + row0 + lax.broadcasted_iota(jnp.int32, (rows, LEVELS), 0), waves)
+                grad_copy(u - PIECES, d).wait()
+
+        for s in range(PAIR):
+            masks = band_masks(own_wave(g, s) + row0 + lax.broadcasted_iota(jnp.int32, (rows, LEVELS), 0), waves)
             for d in range(n_lev):
                 a, _ = level_block(d, i)
+                matrix = mats[:, a].reshape(COV_BANDS * LEVELS, LEVELS)
                 for p in range(2):
                     at = slice(p * LEVELS, (p + 1) * LEVELS)
                     x = own[keep, s, :, at] if d == 0 else back[u, d - 1, s, :, at]
-                    stage[d, pl.ds(p, rows, stride=2), :] = banded_dot(x, masks, vg_ref[a])
-                pieces.at[slot, d].reshape(size, 2 * rows, LEVELS)[s] = stage[d].astype(bf16)
-
-        loop(0, size, one)
+                    stage[s, d, pl.ds(p, rows, stride=2), :] = banded_dot(x, masks, matrix)
+                pieces.at[slot, d].reshape(PAIR, 2 * rows, LEVELS)[s] = stage[s, d].astype(bf16)
+
         for d in range(n_lev):
             grad_copy(u, d).start()
 
-    ahead = RING - 1
-    full_copy().start()
-    for u in range(2):
+    mats_copy().start()
+    for u in range(PIECES):
         for d in range(n_lev):
             x_copy(u, d).start()
+    full_copy().start()
     weight_copy(0).start()
-    enter(n_wave, n_lev)
+    barrier = greet(n_wave, n_lev)
+    mats_copy().wait()
+    for b in range(COV_BANDS):
+        for a in range(variables):
+            mats_t[a, b * LEVELS:(b + 1) * LEVELS, :] = mats[b, a].T
+    pl.semaphore_wait(barrier, n_wave + n_lev - 2)
     for d in lev_others:
         table_copy(0, d).start()
-    loop(0, ahead, vertical)
-    loop(0, lats // 2, build)
+
+    def first(u):
+        vertical(u)
+        send_levels(u)
+
+    loop(0, AHEAD, first)
+    make_order()
 
     def front(u):
         legendre(u)
-        vertical(u + ahead)
-
-        @pl.when(u == 0)
-        def _():
-            loop(lats // 2, lats, build)
-
-    loop(0, units - ahead, front)
-    loop(units - ahead, units, legendre)
+
+        @pl.when(u + AHEAD < units)
+        def _():
+            vertical(u + AHEAD)
+            send_levels(u + AHEAD)
+
+        @pl.when((u >= subs) & (u - subs < lats))
+        def _():
+            build(u - subs)
+
+    loop(0, units, front)
     loop(0, chunks, grid)
-    adjoint_legendre(0)
-
-    def tail(u):
-        adjoint_legendre(u + 1)
-        adjoint_vertical(u)
-
-    loop(0, units - 1, tail)
-    adjoint_vertical(units - 1)
+
+    def last(u):
+        @pl.when(u < units)
+        def _():
+            adjoint_legendre(u)
+
+        @pl.when(u > 0)
+        def _():
+            adjoint_vertical(u - 1)
+
+    loop(0, units + 1, last)
     inc_copy(chunks - 1).wait()
-    for u in range(units - 2, units):
+    for u in range(units - PIECES, units):
         for d in range(n_lev):
             grad_copy(u, d).wait()
-    for u in range(units - RING, units):
+
+    def drain(u):
         for d in lev_others:
-            back_copy(u, d).wait_send()
+            back_copy(units - RING + u, d).wait_send()
+
+    loop(0, RING, drain)
 
 
 def shards_kernel(n_wave, n_lev, control, wave_of_slot, legendre, vertical, points, lat_band, grid_scale, obs_weight):
@@ -494,57 +540,52 @@
     columns = control.shape[4]
     cols = columns // n_lev
     lats, _, longs = obs_weight.shape
-    per = variables // n_lev
-    chunks = members * per
-    size = slots // GROUPS
-    units = chunks * GROUPS
+    chunks = members * variables // n_lev
+    subs = slots // PAIR
+    units = chunks * subs
+    width = 2 * LEVELS
     bf16, f32 = jnp.bfloat16, jnp.float32
-    own_waves = lax.dynamic_slice_in_dim(wave_of_slot, lax.axis_index("wave") * slots, slots)
-    order = wave_of_slot.reshape(n_wave, GROUPS, size).transpose(1, 0, 2).reshape(waves, 1).astype(f32)
-    stack_f = vertical.transpose(1, 0, 3, 2).reshape(variables, COV_BANDS * LEVELS, LEVELS)
-    stack_g = vertical.transpose(1, 0, 2, 3).reshape(variables, COV_BANDS * LEVELS, LEVELS)
-    chooser = (
-        lat_band[:, None] == jnp.arange(grid_scale.shape[0], dtype=jnp.int32)[None, :]
-    ).astype(f32)
-    lat_scale = jnp.dot(chooser, grid_scale, precision=lax.Precision.HIGHEST).T
     vmem = pl.BlockSpec(memory_space=pltpu.VMEM)
     smem = pl.BlockSpec(memory_space=pltpu.SMEM)
     hbm = pl.BlockSpec(memory_space=pl.ANY)
     dma = pltpu.SemaphoreType.DMA
     others = n_lev - 1
-    half = (size, rows, 2 * LEVELS)
-    packet = (units, n_wave, lats, size, 2 * LEVELS)
+    half = (PAIR, rows, width)
     return pl.pallas_call(
         functools.partial(transform_kernel, n_wave, n_lev),
         out_shape=[
             jax.ShapeDtypeStruct((members, lats, cols, longs), bf16),
             jax.ShapeDtypeStruct(control.shape, bf16),
         ],
-        in_specs=[smem, smem, vmem, vmem, vmem, vmem, hbm, hbm, hbm],
+        in_specs=[smem, smem, smem, vmem, hbm, hbm, hbm, hbm],
         out_specs=[hbm, hbm],
         scratch_shapes=[
             pltpu.VMEM((n_lev, *legendre.shape), bf16),
-            pltpu.VMEM((2, n_lev, size, rows, 2, LEVELS), bf16),
+            pltpu.VMEM(vertical.shape, bf16),
+            pltpu.VMEM((variables, COV_BANDS * LEVELS, LEVELS), bf16),
+            pltpu.VMEM((waves, LEVELS), f32),
+            pltpu.VMEM((PIECES, n_lev, PAIR, rows, 2, LEVELS), bf16),
             pltpu.VMEM((RING, *half), bf16),
             pltpu.VMEM((RING, others, *half), bf16),
             pltpu.VMEM((units, others, *half), bf16),
             pltpu.VMEM((units, others, *half), bf16),
-            pltpu.VMEM((size * n_wave * lats, 2 * LEVELS), f32),
-            pltpu.VMEM(packet, bf16),
-            pltpu.VMEM(packet, bf16),
-            pltpu.VMEM(packet, bf16),
+            pltpu.VMEM((2, n_wave * lats * PAIR, LEVELS), f32),
+            pltpu.VMEM((chunks, subs, 2, n_wave, lats, PAIR, LEVELS), bf16),
+            pltpu.VMEM((chunks, 2, lats, subs, n_wave, PAIR, LEVELS), bf16),
+            pltpu.VMEM((chunks, 2, lats, subs, n_wave, PAIR, LEVELS), bf16),
+            pltpu.VMEM((units, 2, n_wave, lats, PAIR, LEVELS), bf16),
             pltpu.VMEM((lats, 2 * waves, longs), bf16),
             pltpu.VMEM((lats, LEVELS, longs), bf16),
             pltpu.VMEM((lats, LEVELS, longs), bf16),
-            pltpu.VMEM((n_lev, 2 * rows, LEVELS), f32),
-            dma, dma((2, n_lev)), dma, dma, dma((2, n_lev)),
-            dma((GROUPS, others)), dma((GROUPS, others)),
+            pltpu.VMEM((PAIR, n_lev, 2 * rows, LEVELS), f32),
+            dma, dma, dma((PIECES, n_lev)), dma, dma, dma((PIECES, n_lev)),
+            dma((subs, others)), dma((subs, others)),
             dma((units, others)), dma((units, others)), dma((units, others)), dma((units, others)),
-            dma((units, n_wave - 1)), dma((units, n_wave - 1)), dma((units, n_wave - 1)), dma((units, n_wave - 1)),
+            dma((units,)), dma((units,)), dma((units,)), dma((units,)),
         ],
         compiler_params=pltpu.CompilerParams(collective_id=0, has_side_effects=True, vmem_limit_bytes=VMEM_BYTES),
         name="transform",
-    )(own_waves, points, order, lat_scale, stack_f, stack_g, control, legendre, obs_weight)
+    )(wave_of_slot, points, lat_band, grid_scale, vertical, control, legendre, obs_weight)
 
 
 def shards(n_wave, n_lev, *arrays):

time: 451 us -> 400 us (0.89)
  Pallas kernels: 426 us -> 383 us
  local copies, waits for them, and re-layouts: 21.8 us -> 15.7 us
    pallas_call x1, Pallas kernels: 426 us -> 383 us  [shards_kernel(): pl.pallas_call(functools.partial(transform_kernel, n_wave, n_lev), out_sh...]
    unnamed x4 -> x2, local copies, waits for them, and re-layouts: 15.7 us -> 15.7 us
where the time goes in v2:
time: 400 us; the launch traced here: 399 us
  Pallas kernels  383 us (96%)
  local copies, waits for them, and re-layouts  15.7 us (4%)
    pallas_call x1, Pallas kernels, shards_kernel(): pl.pallas_call(functools.partial(transform_kernel, n_wave, n_lev), out_sh...  383 us
    unnamed x2, local copies, waits for them, and re-layouts  15.7 us

profile of v2, /device:TPU:29, one launch (start us, length us, event | category | flops | bytes accessed | tf_op | source)
XLA Modules:
  0.0 399.4 jit_solution(1644256702182136659)
XLA Ops:
  0.6 383.0 %transform.1 = (bf16[2,16,256,512]{3,2,1,0:T(8,128)(2,1)}, bf16[2,16,128,2,512]{4,3,2,1,0:T(2,128)(2,1)}) custom-call(s32[256]{0:T(256)} %waves_ref.1, s32[16]{0:T(128)} %points_ref.1, s32[16]{0:T(128)} %band_ref.1, f32[8,256]{1,0:T(8,128)} %grid_scale_ref.1, bf16[4,4,128,128]{3,2,1,0:T(8,128)(2,1)} %v_ref.1, bf16[2,16,128,2,512]{4,3,2,1,0:T(2,128)(2,1)} %x_ref.1, ...), custom_call_target="tpu_custom_call" | custom-call | tf_op jit(solution)/shard_map/transform/pallas_call | solution.py:554
  383.7 7.7 %copy.12 = bf16[2,16,256,512]{3,2,1,0:T(8,128)(2,1)} copy(bf16[2,16,256,512]{3,2,1,0:T(8,128)(2,1)} %get-tuple-element.4) | data formatting | bytes 16777216
  391.3 8.0 %copy.13 = bf16[2,16,128,2,512]{4,3,2,1,0:T(2,128)(2,1)} copy(bf16[2,16,128,2,512]{4,3,2,1,0:T(2,128)(2,1)} %get-tuple-element.5) | data formatting | bytes 16777216

commit v3 on v2

--- a/solution.py
+++ b/solution.py
@@ -163,10 +163,10 @@
     lax.fori_loop(first, last, step, 0)
 
 
-def transform_kernel(n_wave, n_lev, waves_ref, points_ref, band_ref, grid_scale_ref, v_ref, x_ref, l_ref, weight_ref,
+def transform_kernel(n_wave, n_lev, waves_hbm, points_hbm, band_hbm, scale_hbm, v_ref, x_ref, l_ref, weight_ref,
                      inc_ref, grad_ref,
-                     full, mats, mats_t, order, pieces, own, away, spec, back, coef, wsend, asend, land, aland, table, wbuf, ibuf, stage,
-                     full_sem, mats_sem, x_sem, weight_sem, inc_sem, grad_sem, l_send, l_recv, f_send, f_recv, b_send, b_recv,
+                     waves_ref, points_ref, band_ref, grid_scale_ref, full, mats, mats_t, order, pieces, own, away, spec, back, coef, wsend, asend, land, aland, table, wbuf, ibuf, stage,
+                     small_sem, full_sem, mats_sem, x_sem, weight_sem, inc_sem, grad_sem, l_send, l_recv, f_send, f_recv, b_send, b_recv,
                      w_send, w_recv, a_send, a_recv):
     members, slots, rows = x_ref.shape[:3]
     variables = v_ref.shape[1]
@@ -216,6 +216,10 @@
 
     def full_copy():
         return pltpu.make_async_copy(l_ref, full.at[me_l], full_sem)
+
+    def small_copies():
+        pairs = [(waves_hbm, waves_ref), (scale_hbm, grid_scale_ref), (points_hbm, points_ref), (band_hbm, band_ref)]
+        return [pltpu.make_async_copy(src, dst, small_sem.at[k]) for k, (src, dst) in enumerate(pairs)]
 
     def mats_copy():
         return pltpu.make_async_copy(v_ref, mats, mats_sem)
@@ -420,6 +424,10 @@
         def _():
             weight_copy(q + 1).start()
 
+    def project(d, g, s, field):
+        table_part = full[lax.rem(me_l + d, n_lev), g * PAIR + s]
+        return jnp.dot(table_part, field, preferred_element_type=f32).astype(bf16)
+
     def adjoint_legendre(u):
         _, g, e, i = where_is(u)
         keep = lax.rem(u, RING)
@@ -437,43 +445,45 @@
 
         for p in range(2):
             coef[p] = aland.at[u, p].reshape(lat_all * PAIR, LEVELS)[...].astype(f32)
+        fields = []
         for s in range(PAIR):
             field = jnp.concatenate(
                 [coef[p, pl.ds(s, lat_all, stride=PAIR), :].astype(bf16) for p in range(2)], axis=1)
-            for d in lev_order:
-                y = jnp.dot(full[lax.rem(me_l + d, n_lev), g * PAIR + s], field, preferred_element_type=f32).astype(bf16)
-                if d == 0:
-                    own[keep, s] = y
-                else:
-                    away[keep, d - 1, s] = y
+            fields.append(field)
+            for d in lev_others:
+                away[keep, d - 1, s] = project(d, g, s, field)
         for d in lev_others:
             back_copy(u, d).start()
+        for s in range(PAIR):
+            own[keep, s] = project(0, g, s, fields[s])
 
     def adjoint_vertical(u):
         _, g, e, i = where_is(u)
         slot, keep = lax.rem(u, PIECES), lax.rem(u, RING)
-        for d in lev_others:
-            back_copy(u, d).wait_recv()
-
         @pl.when(u >= PIECES)
         def _():
             for d in range(n_lev):
                 grad_copy(u - PIECES, d).wait()
 
-        for s in range(PAIR):
-            masks = band_masks(own_wave(g, s) + row0 + lax.broadcasted_iota(jnp.int32, (rows, LEVELS), 0), waves)
-            for d in range(n_lev):
-                a, _ = level_block(d, i)
-                matrix = mats[:, a].reshape(COV_BANDS * LEVELS, LEVELS)
+        masks = [
+            band_masks(own_wave(g, s) + row0 + lax.broadcasted_iota(jnp.int32, (rows, LEVELS), 0), waves)
+            for s in range(PAIR)
+        ]
+        for d in range(n_lev):
+            if d > 0:
+                back_copy(u, d).wait_recv()
+            a, _ = level_block(d, i)
+            matrix = mats[:, a].reshape(COV_BANDS * LEVELS, LEVELS)
+            for s in range(PAIR):
                 for p in range(2):
                     at = slice(p * LEVELS, (p + 1) * LEVELS)
                     x = own[keep, s, :, at] if d == 0 else back[u, d - 1, s, :, at]
-                    stage[s, d, pl.ds(p, rows, stride=2), :] = banded_dot(x, masks, matrix)
+                    stage[s, d, pl.ds(p, rows, stride=2), :] = banded_dot(x, masks[s], matrix)
                 pieces.at[slot, d].reshape(PAIR, 2 * rows, LEVELS)[s] = stage[s, d].astype(bf16)
-
-        for d in range(n_lev):
             grad_copy(u, d).start()
 
+    for copy in small_copies():
+        copy.start()
     mats_copy().start()
     for u in range(PIECES):
         for d in range(n_lev):
@@ -485,6 +495,8 @@
     for b in range(COV_BANDS):
         for a in range(variables):
             mats_t[a, b * LEVELS:(b + 1) * LEVELS, :] = mats[b, a].T
+    for copy in small_copies():
+        copy.wait()
     pl.semaphore_wait(barrier, n_wave + n_lev - 2)
     for d in lev_others:
         table_copy(0, d).start()
@@ -494,7 +506,6 @@
         send_levels(u)
 
     loop(0, AHEAD, first)
-    make_order()
 
     def front(u):
         legendre(u)
@@ -503,6 +514,10 @@
         def _():
             vertical(u + AHEAD)
             send_levels(u + AHEAD)
+
+        @pl.when(u == subs - 1)
+        def _():
+            make_order()
 
         @pl.when((u >= subs) & (u - subs < lats))
         def _():
@@ -531,6 +546,46 @@
             back_copy(units - RING + u, d).wait_send()
 
     loop(0, RING, drain)
+
+
+def settle_kernel(inc_ref, grad_ref, inc_out, grad_out, a, b, a_in, a_out, b_in, b_out):
+    def moves(i):
+        return [
+            (pltpu.make_async_copy(inc_ref.at[:, i], a.at[i], a_in.at[i]),
+             pltpu.make_async_copy(a.at[i], inc_out.at[:, i], a_out.at[i])),
+            (pltpu.make_async_copy(grad_ref.at[:, i], b.at[i], b_in.at[i]),
+             pltpu.make_async_copy(b.at[i], grad_out.at[:, i], b_out.at[i])),
+        ]
+
+    steps = a.shape[0]
+    stages = [moves(i) for i in range(steps)]
+    for pairs in stages:
+        for first, _ in pairs:
+            first.start()
+    for pairs in stages:
+        for first, then in pairs:
+            first.wait()
+            then.start()
+    for pairs in stages:
+        for _, then in pairs:
+            then.wait()
+
+
+def settle(increment, gradient):
+    hbm = pl.BlockSpec(memory_space=pl.ANY)
+    dma = pltpu.SemaphoreType.DMA
+    shapes = [increment.shape, gradient.shape]
+    steps = increment.shape[1]
+    kept = [pltpu.VMEM((steps, s[0], *s[2:]), jnp.bfloat16) for s in shapes]
+    return pl.pallas_call(
+        settle_kernel,
+        out_shape=[jax.ShapeDtypeStruct(s, jnp.bfloat16) for s in shapes],
+        in_specs=[hbm, hbm],
+        out_specs=[hbm, hbm],
+        scratch_shapes=[*kept, *[dma((steps,))] * 4],
+        compiler_params=pltpu.CompilerParams(vmem_limit_bytes=VMEM_BYTES),
+        name="settle",
+    )(increment, gradient)
 
 
 def shards_kernel(n_wave, n_lev, control, wave_of_slot, legendre, vertical, points, lat_band, grid_scale, obs_weight):
@@ -545,21 +600,23 @@
     units = chunks * subs
     width = 2 * LEVELS
     bf16, f32 = jnp.bfloat16, jnp.float32
-    vmem = pl.BlockSpec(memory_space=pltpu.VMEM)
-    smem = pl.BlockSpec(memory_space=pltpu.SMEM)
     hbm = pl.BlockSpec(memory_space=pl.ANY)
     dma = pltpu.SemaphoreType.DMA
     others = n_lev - 1
     half = (PAIR, rows, width)
-    return pl.pallas_call(
+    results = pl.pallas_call(
         functools.partial(transform_kernel, n_wave, n_lev),
         out_shape=[
             jax.ShapeDtypeStruct((members, lats, cols, longs), bf16),
             jax.ShapeDtypeStruct(control.shape, bf16),
         ],
-        in_specs=[smem, smem, smem, vmem, hbm, hbm, hbm, hbm],
+        in_specs=[hbm] * 8,
         out_specs=[hbm, hbm],
         scratch_shapes=[
+            pltpu.SMEM(wave_of_slot.shape, jnp.int32),
+            pltpu.SMEM(points.shape, jnp.int32),
+            pltpu.SMEM(lat_band.shape, jnp.int32),
+            pltpu.VMEM(grid_scale.shape, f32),
             pltpu.VMEM((n_lev, *legendre.shape), bf16),
             pltpu.VMEM(vertical.shape, bf16),
             pltpu.VMEM((variables, COV_BANDS * LEVELS, LEVELS), bf16),
@@ -578,7 +635,7 @@
             pltpu.VMEM((lats, LEVELS, longs), bf16),
             pltpu.VMEM((lats, LEVELS, longs), bf16),
             pltpu.VMEM((PAIR, n_lev, 2 * rows, LEVELS), f32),
-            dma, dma, dma((PIECES, n_lev)), dma, dma, dma((PIECES, n_lev)),
+            dma((4,)), dma, dma, dma((PIECES, n_lev)), dma, dma, dma((PIECES, n_lev)),
             dma((subs, others)), dma((subs, others)),
             dma((units, others)), dma((units, others)), dma((units, others)), dma((units, others)),
             dma((units,)), dma((units,)), dma((units,)), dma((units,)),
@@ -586,6 +643,7 @@
         compiler_params=pltpu.CompilerParams(collective_id=0, has_side_effects=True, vmem_limit_bytes=VMEM_BYTES),
         name="transform",
     )(wave_of_slot, points, lat_band, grid_scale, vertical, control, legendre, obs_weight)
+    return tuple(settle(*results))
 
 
 def shards(n_wave, n_lev, *arrays):

time: 400 us -> 395 us (0.988)
  local copies, waits for them, and re-layouts: 15.7 us -> 0 us
  Pallas kernels: 383 us -> 393 us
    unnamed x2 -> x0, local copies, waits for them, and re-layouts: 15.7 us -> none
    pallas_call x0 -> x1, Pallas kernels: none -> 12.3 us  [settle(): pl.pallas_call(settle_kernel, out_shape=[jax.ShapeDtypeStruct(s, jnp.bflo...]
where the time goes in v3:
time: 395 us; the launch traced here: 394 us
  Pallas kernels  393 us (99%)
    pallas_call x1, Pallas kernels, shards_kernel(): pl.pallas_call(functools.partial(transform_kernel, n_wave, n_lev), out_sh...  381 us
    pallas_call x1, Pallas kernels, settle(): pl.pallas_call(settle_kernel, out_shape=[jax.ShapeDtypeStruct(s, jnp.bflo...  12.3 us

profile of v3, /device:TPU:29, one launch (start us, length us, event | category | flops | bytes accessed | tf_op | source)
XLA Modules:
  0.0 394.0 jit_solution(9218942679557741812)
XLA Ops:
  0.6 381.0 %transform.1 = (bf16[2,16,256,512]{3,2,1,0:T(8,128)(2,1)}, bf16[2,16,128,2,512]{4,3,2,1,0:T(2,128)(2,1)}) custom-call(s32[256]{0:T(256)} %waves_hbm.1, s32[16]{0:T(128)} %points_hbm.1, s32[16]{0:T(128)} %band_hbm.1, f32[8,256]{1,0:T(8,128)} %scale_hbm.1, bf16[4,4,128,128]{3,2,1,0:T(8,128)(2,1)} %v_ref.1, bf16[2,16,128,2,512]{4,3,2,1,0:T(2,128)(2,1)} %x_ref.1, ...), custom_call_target="tpu_custom_call" | custom-call | tf_op jit(solution)/shard_map/transform/pallas_call | solution.py:607
  381.6 12.3 %settle.1 = (bf16[2,16,256,512]{3,2,1,0:T(8,128)(2,1)}, bf16[2,16,128,2,512]{4,3,2,1,0:T(2,128)(2,1)}) custom-call(bf16[2,16,256,512]{3,2,1,0:T(8,128)(2,1)} %get-tuple-element.4.inc_ref, bf16[2,16,128,2,512]{4,3,2,1,0:T(2,128)(2,1)} %get-tuple-element.5.grad_ref), custom_call_target="tpu_custom_call" | custom-call | tf_op jit(solution)/shard_map/settle/pallas_call | solution.py:580

commit v4 on v3

--- a/solution.py
+++ b/solution.py
@@ -231,18 +231,21 @@
             send_sem=l_send.at[g, d - 1], recv_sem=l_recv.at[g, d - 1],
             device_id=(me_w, peer), device_id_type=MESH)
 
-    def lev_copy(u, d, target, send_sem, recv_sem):
+    def lev_copy(u, d, p, target, send_sem, recv_sem):
         peer = lax.rem(me_l + d, n_lev)
+        at = pl.ds(p * LEVELS, LEVELS)
         return pltpu.make_async_remote_copy(
-            src_ref=away.at[lax.rem(u, RING), d - 1], dst_ref=target.at[u, n_lev - d - 1],
-            send_sem=send_sem.at[u, d - 1], recv_sem=recv_sem.at[u, d - 1],
+            src_ref=away.at[lax.rem(u, RING), d - 1, :, :, at], dst_ref=target.at[u, n_lev - d - 1, :, :, at],
+            send_sem=send_sem.at[u, d - 1, p], recv_sem=recv_sem.at[u, d - 1, p],
             device_id=(me_w, peer), device_id_type=MESH)
 
-    def out_copy(u, d):
-        return lev_copy(u, d, spec, f_send, f_recv)
-
-    def back_copy(u, d):
-        return lev_copy(u, d, back, b_send, b_recv)
+    def out_copy(u, d, p):
+        return lev_copy(u, d, p, spec, f_send, f_recv)
+
+    def back_copy(u, d, p):
+        return lev_copy(u, d, p, back, b_send, b_recv)
+
+    lev_parts = [(d, p) for p in range(2) for d in range(1, n_lev)]
 
     def remote(src, dst, send_sem, recv_sem, d):
         return pltpu.make_async_remote_copy(
@@ -258,6 +261,21 @@
         q, g, _, _ = where_is(u)
         most = pl.ds(0, n_wave - 1)
         return remote(wsend.at[q, g, :, most], land.at[q, :, :, g, most], w_send.at[u], w_recv.at[u], 1)
+
+    def land_half(u, p, d):
+        q, g, _, _ = where_is(u)
+        peer = lax.rem(me_w + d, n_wave)
+        return remote(wsend.at[q, g, p, peer], land.at[q, p, :, g, me_w], w_send.at[u], w_recv.at[u], d)
+
+    def aland_half(p, d):
+        peer = lax.rem(me_w + d, n_wave)
+        return remote(asend.at[chunks - 1, p, :, subs - 1, peer], aland.at[units - 1, p, me_w],
+                      a_send.at[units - 1 + p], a_recv.at[units - 1 + p], d)
+
+    def aland_half_all(p):
+        most = pl.ds(0, n_wave - 1)
+        return remote(asend.at[chunks - 1, p, :, subs - 1, most], aland.at[units - 1, p, most],
+                      a_send.at[units - 1 + p], a_recv.at[units - 1 + p], 1)
 
     def aland_copy(u, d):
         q, g, _, _ = where_is(u)
@@ -283,8 +301,8 @@
 
         @pl.when(u >= RING)
         def _():
-            for d in lev_others:
-                out_copy(u - RING, d).wait_send()
+            for d, p in lev_parts:
+                out_copy(u - RING, d, p).wait_send()
 
         for s in range(PAIR):
             total = own_wave(g, s) + row0 + lax.div(lax.broadcasted_iota(jnp.int32, (2 * rows, LEVELS), 0), 2)
@@ -306,8 +324,8 @@
                 x_copy(u + PIECES, d).start()
 
     def send_levels(u):
-        for d in lev_others:
-            out_copy(u, d).start()
+        for d, p in lev_parts:
+            out_copy(u, d, p).start()
 
         @pl.when(u + 1 < subs)
         def _():
@@ -327,22 +345,28 @@
             for d in lev_others:
                 table_copy(u, d).wait()
 
-        for d in lev_others:
-            out_copy(u, d).wait_recv()
-
-        for s in range(PAIR):
-            fields, tables = [], []
-            for d in range(n_lev):
-                fields.append(own[keep, s] if d == 0 else spec[u, d - 1, s])
-                tables.append(full[lax.rem(me_l + d, n_lev), g * PAIR + s])
-            value = lax.dot_general(
-                jnp.concatenate(tables, axis=0), jnp.concatenate(fields, axis=0),
-                (((0,), (0,)), ((), ())), preferred_element_type=f32)
-            for p in range(2):
-                coef[p, pl.ds(s, lat_all, stride=PAIR), :] = value[:, p * LEVELS:(p + 1) * LEVELS]
         for p in range(2):
+            at = slice(p * LEVELS, (p + 1) * LEVELS)
+            for d in lev_others:
+                out_copy(u, d, p).wait_recv()
+            for s in range(PAIR):
+                fields, tables = [], []
+                for d in range(n_lev):
+                    fields.append(own[keep, s, :, at] if d == 0 else spec[u, d - 1, s, :, at])
+                    tables.append(full[lax.rem(me_l + d, n_lev), g * PAIR + s])
+                coef[p, pl.ds(s, lat_all, stride=PAIR), :] = lax.dot_general(
+                    jnp.concatenate(tables, axis=0), jnp.concatenate(fields, axis=0),
+                    (((0,), (0,)), ((), ())), preferred_element_type=f32)
             wsend.at[q, g, p].reshape(lat_all * PAIR, LEVELS)[...] = coef[p].astype(bf16)
-        loop(1, n_wave, lambda d: land_copy(u, d).start())
+
+            @pl.when(u == 0)
+            def _():
+                loop(1, n_wave, lambda d: land_half(u, p, d).start())
+
+        @pl.when(u > 0)
+        def _():
+            loop(1, n_wave, lambda d: land_copy(u, d).start())
+
         land[q, :, :, g, me_w] = wsend[q, g, :, me_w]
 
     def make_order():
@@ -414,7 +438,16 @@
 
         def send(g):
             u = q * subs + g
-            loop(1, n_wave, lambda d: aland_copy(u, d).start())
+
+            @pl.when(u < units - 1)
+            def _():
+                loop(1, n_wave, lambda d: aland_copy(u, d).start())
+
+            @pl.when(u == units - 1)
+            def _():
+                for p in range(2):
+                    loop(1, n_wave, lambda d: aland_half(p, d).start())
+
             aland[u, :, me_w] = asend[q, :, :, g, me_w]
 
         loop(0, subs, send)
@@ -431,31 +464,36 @@
     def adjoint_legendre(u):
         _, g, e, i = where_is(u)
         keep = lax.rem(u, RING)
-        aland_all(u).wait()
+
+        @pl.when(u < units - 1)
+        def _():
+            aland_all(u).wait()
 
         @pl.when(u < RING)
         def _():
+            for d, p in lev_parts:
+                out_copy(u + units - RING, d, p).wait_send()
+
+        @pl.when(u >= RING)
+        def _():
+            for d, p in lev_parts:
+                back_copy(u - RING, d, p).wait_send()
+
+        for p in range(2):
+            at = slice(p * LEVELS, (p + 1) * LEVELS)
+
+            @pl.when(u == units - 1)
+            def _():
+                aland_half_all(p).wait()
+
+            coef[p] = aland.at[u, p].reshape(lat_all * PAIR, LEVELS)[...].astype(f32)
+            fields = [coef[p, pl.ds(s, lat_all, stride=PAIR), :].astype(bf16) for s in range(PAIR)]
             for d in lev_others:
-                out_copy(u + units - RING, d).wait_send()
-
-        @pl.when(u >= RING)
-        def _():
-            for d in lev_others:
-                back_copy(u - RING, d).wait_send()
-
-        for p in range(2):
-            coef[p] = aland.at[u, p].reshape(lat_all * PAIR, LEVELS)[...].astype(f32)
-        fields = []
-        for s in range(PAIR):
-            field = jnp.concatenate(
-                [coef[p, pl.ds(s, lat_all, stride=PAIR), :].astype(bf16) for p in range(2)], axis=1)
-            fields.append(field)
-            for d in lev_others:
-                away[keep, d - 1, s] = project(d, g, s, field)
-        for d in lev_others:
-            back_copy(u, d).start()
-        for s in range(PAIR):
-            own[keep, s] = project(0, g, s, fields[s])
+                for s in range(PAIR):
+                    away[keep, d - 1, s, :, at] = project(d, g, s, fields[s])
+                back_copy(u, d, p).start()
+            for s in range(PAIR):
+                own[keep, s, :, at] = project(0, g, s, fields[s])
 
     def adjoint_vertical(u):
         _, g, e, i = where_is(u)
@@ -470,15 +508,16 @@
             for s in range(PAIR)
         ]
         for d in range(n_lev):
-            if d > 0:
-                back_copy(u, d).wait_recv()
             a, _ = level_block(d, i)
             matrix = mats[:, a].reshape(COV_BANDS * LEVELS, LEVELS)
-            for s in range(PAIR):
-                for p in range(2):
+            for p in range(2):
+                if d > 0:
+                    back_copy(u, d, p).wait_recv()
+                for s in range(PAIR):
                     at = slice(p * LEVELS, (p + 1) * LEVELS)
                     x = own[keep, s, :, at] if d == 0 else back[u, d - 1, s, :, at]
                     stage[s, d, pl.ds(p, rows, stride=2), :] = banded_dot(x, masks[s], matrix)
+            for s in range(PAIR):
                 pieces.at[slot, d].reshape(PAIR, 2 * rows, LEVELS)[s] = stage[s, d].astype(bf16)
             grad_copy(u, d).start()
 
@@ -542,8 +581,8 @@
             grad_copy(u, d).wait()
 
     def drain(u):
-        for d in lev_others:
-            back_copy(units - RING + u, d).wait_send()
+        for d, p in lev_parts:
+            back_copy(units - RING + u, d, p).wait_send()
 
     loop(0, RING, drain)
 
@@ -637,8 +676,8 @@
             pltpu.VMEM((PAIR, n_lev, 2 * rows, LEVELS), f32),
             dma((4,)), dma, dma, dma((PIECES, n_lev)), dma, dma, dma((PIECES, n_lev)),
             dma((subs, others)), dma((subs, others)),
-            dma((units, others)), dma((units, others)), dma((units, others)), dma((units, others)),
-            dma((units,)), dma((units,)), dma((units,)), dma((units,)),
+            *[dma((units, others, 2))] * 4,
+            dma((units,)), dma((units,)), dma((units + 1,)), dma((units + 1,)),
         ],
         compiler_params=pltpu.CompilerParams(collective_id=0, has_side_effects=True, vmem_limit_bytes=VMEM_BYTES),
         name="transform",

time: 395 us -> 397 us (level)
  no operation moved by 1% of the time
where the time goes in v4:
time: 397 us; the launch traced here: 395 us
  Pallas kernels  395 us (99%)
    pallas_call x1, Pallas kernels, shards_kernel(): pl.pallas_call(functools.partial(transform_kernel, n_wave, n_lev), out_sh...  382 us
    pallas_call x1, Pallas kernels, settle(): pl.pallas_call(settle_kernel, out_shape=[jax.ShapeDtypeStruct(s, jnp.bflo...  12.3 us

profile of v4, /device:TPU:29, one launch (start us, length us, event | category | flops | bytes accessed | tf_op | source)
XLA Modules:
  0.0 395.3 jit_solution(6648021842767119917)
XLA Ops:
  0.6 382.3 %transform.1 = (bf16[2,16,256,512]{3,2,1,0:T(8,128)(2,1)}, bf16[2,16,128,2,512]{4,3,2,1,0:T(2,128)(2,1)}) custom-call(s32[256]{0:T(256)} %waves_hbm.1, s32[16]{0:T(128)} %points_hbm.1, s32[16]{0:T(128)} %band_hbm.1, f32[8,256]{1,0:T(8,128)} %scale_hbm.1, bf16[4,4,128,128]{3,2,1,0:T(8,128)(2,1)} %v_ref.1, bf16[2,16,128,2,512]{4,3,2,1,0:T(2,128)(2,1)} %x_ref.1, ...), custom_call_target="tpu_custom_call" | custom-call | tf_op jit(solution)/shard_map/transform/pallas_call | solution.py:646
  383.0 12.3 %settle.1 = (bf16[2,16,256,512]{3,2,1,0:T(8,128)(2,1)}, bf16[2,16,128,2,512]{4,3,2,1,0:T(2,128)(2,1)}) custom-call(bf16[2,16,256,512]{3,2,1,0:T(8,128)(2,1)} %get-tuple-element.4.inc_ref, bf16[2,16,128,2,512]{4,3,2,1,0:T(2,128)(2,1)} %get-tuple-element.5.grad_ref), custom_call_target="tpu_custom_call" | custom-call | tf_op jit(solution)/shard_map/settle/pallas_call | solution.py:619
